TPU v7x, 128 devices: a whole 4x4x4 slice. The times are simulated.
128 devices in a mesh: group: 8 (over y, core), peer: 16 (over z, x).
Axes of the slice: x: 4, y: 4, z: 4, core: 2. Of those that a mesh axis runs over, the one named last changes fastest.
Arguments:
- states: float32 [41, 4194304], P(None, ('group', 'peer')), may hold values from -6 to 6
- block_part: int32 [32768], P(('group', 'peer')), may hold values from 0 to 127, as said below
- tile_perm: int32 [32768, 128], P(('group', 'peer')), may hold values from 0 to 127, each once within a row
- half_volt: float32 [40], replicated, may hold values from -4 to 4
- steepness: float32 [40], replicated, may hold values from 0.5 to 4
- gate_rate: float32 [40], replicated, may hold values from 0.1 to 1
- conductance: float32 [40], replicated, may hold values from 0.005 to 0.08
- reversal: float32 [40], replicated, may hold values from -6 to 6
Outputs:
- regrouped: float32 [41, 4194304], P(None, ('group', 'peer'))
Inputs may be any that keep to these rules, and one draw needn't show every extreme that they name: `block_part`: every partition holds exactly 256 blocks. Within each slab of 256 consecutive global blocks no partition holds more than 4 blocks; every slab has exactly 4 blocks of some partition, and every partition has exactly 4 blocks in some slab.
All inputs are finite; a program needn't handle non-finite values.
Results may differ from a plain program's by a relative error of at most 0.0001.
Values sent between devices are 32-bit elements; how exact they have to be, the bound alone decides.
A program may use at most 192 MiB of HBM per device.

v0:
```python
import jax
import jax.numpy as jnp
from jax import lax
from jax.sharding import Mesh
from jax.sharding import PartitionSpec as P

GROUP_PEER = ("group_0", "group_1", "peer_0", "peer_1")


time_step = 0.25


def neutral_like(value, identity):
    return jnp.broadcast_to(jnp.asarray(identity, value.dtype), value.shape)


def prefix_by_axis(value, axes, combine, identity):
    before = start = neutral_like(value, identity)
    subtotal = value
    for axis in reversed(axes):
        length, here = (lax.axis_size(axis), lax.axis_index(axis))
        pieces = lax.all_gather(subtotal, axis)
        inside, subtotal = (start, start)
        for k in range(length):
            passed = k < here
            subtotal = combine(subtotal, pieces[k])
            inside = jnp.where(passed, subtotal, inside)
        before = combine(inside, before)
    return before


def advance(state_rows, half_volt, steepness, gate_rate, conductance, reversal):
    voltage = state_rows[0:1]
    gate_vals = state_rows[1:]
    steady = jax.nn.sigmoid((voltage - half_volt[:, None]) * steepness[:, None])
    damping = jnp.exp(-gate_rate[:, None] * (1.0 + jax.nn.sigmoid(voltage)))
    gate_vals = steady + (gate_vals - steady) * damping
    current = jnp.sum(
        conductance[:, None] * gate_vals * (voltage - reversal[:, None]), axis=0, keepdims=True
    )
    voltage = voltage - time_step * current
    return jnp.concatenate([voltage, gate_vals], axis=0)


def add_counts(earlier, later):
    return earlier + later


def on_device(
    states, block_part, tile_perm, half_volt, steepness, gate_rate, conductance, reversal
):
    devices = lax.axis_size(GROUP_PEER)
    local_blocks = block_part.shape[0]
    tile_width = tile_perm.shape[1]
    width = states.shape[0]
    capacity = 2 * local_blocks // devices
    partitions = jnp.arange(devices, dtype=jnp.int32)
    onehot = (block_part[:, None] == partitions[None, :]).astype(jnp.int32)
    counts = jnp.sum(onehot, axis=0, dtype=jnp.int32)
    earlier = prefix_by_axis(counts, GROUP_PEER, add_counts, jnp.zeros_like(counts))
    rank_in = jnp.sum(
        (jnp.cumsum(onehot, axis=0, dtype=jnp.int32) - onehot) * onehot, axis=1, dtype=jnp.int32
    )
    local_index = jnp.sum(onehot * earlier[None, :], axis=1, dtype=jnp.int32) + rank_in
    slot_index = block_part * capacity + rank_in
    requests = jnp.full((devices * capacity,), -1, jnp.int32).at[slot_index].set(local_index)
    requests = requests.reshape(devices, capacity)
    advanced = advance(states, half_volt, steepness, gate_rate, conductance, reversal)
    advanced = advanced.reshape(width, local_blocks, tile_width)
    wanted = lax.all_to_all(requests, GROUP_PEER, split_axis=0, concat_axis=0, tiled=True)
    picked = jnp.maximum(wanted, 0).reshape(-1)
    served = jnp.take(advanced, picked, axis=1)
    arrived = lax.all_to_all(
        served.reshape(width, wanted.shape[0], wanted.shape[1], tile_width),
        GROUP_PEER,
        split_axis=1,
        concat_axis=1,
        tiled=True,
    )
    flat_cols = (slot_index[:, None] * tile_width + tile_perm).reshape(-1)
    return jnp.take(arrived.reshape(width, devices * capacity * tile_width), flat_cols, axis=1)


def solution(mesh):
    finer = Mesh(mesh.devices.reshape(4, 2, 4, 4), ("group_0", "group_1", "peer_0", "peer_1"))
    placed = (P(None, GROUP_PEER), P(GROUP_PEER), P(GROUP_PEER, None), P(), P(), P(), P(), P())
    return jax.shard_map(
        on_device, mesh=finer, in_specs=placed, out_specs=P(None, GROUP_PEER), check_vma=False
    )
```

profile of v0, /device:TPU:5, one launch (start us, length us, event | category | flops | bytes accessed | tf_op | source)
XLA Modules:
  0.0 405.4 jit_solution(9539851589758769615)
XLA Ops:
  0.0 0.8 convert_reduce_fusion
  0.8 5.5 %all-gather.1 = s32[4,1,128]{2,1,0:T(1,128)S(1)} all-gather(s32[1,1,128]{2,1,0:T(1,128)S(1)} %bitcast.70), channel_id=2, replica_groups=mesh['group_0'=4,'group_1'=2,'peer_0'=4,'peer_1'=4] {'peer_1'}, dimensions={0}, use_global_device_ids=true | all-gather | bytes 2560 | tf_op jit(solution)/shard_map/all_gather | solution.py:22
  6.3 9.0 %all-gather.2 = s32[4,1,128]{2,1,0:T(1,128)S(1)} all-gather(s32[1,1,128]{2,1,0:T(1,128)S(1)} %slice_add_fusion.7), channel_id=1, replica_groups=mesh['group_0'=4,'group_1'=2,'peer_0'=4,'peer_1'=4] {'peer_0'}, dimensions={0}, use_global_device_ids=true | all-gather | bytes 2560 | tf_op jit(solution)/shard_map/all_gather | solution.py:22
  15.3 6.2 %all-gather.3 = s32[2,1,128]{2,1,0:T(1,128)S(1)} all-gather(s32[1,1,128]{2,1,0:T(1,128)S(1)} %slice_add_fusion.4), channel_id=1, replica_groups=mesh['group_0'=4,'group_1'=2,'peer_0'=4,'peer_1'=4] {'group_1'}, dimensions={0}, use_global_device_ids=true | all-gather | bytes 1536 | tf_op jit(solution)/shard_map/all_gather | solution.py:22
  21.5 7.9 %all-gather.4 = s32[4,1,128]{2,1,0:T(1,128)S(1)} all-gather(s32[1,1,128]{2,1,0:T(1,128)S(1)} %slice_add_fusion.3), channel_id=1, replica_groups=mesh['group_0'=4,'group_1'=2,'peer_0'=4,'peer_1'=4] {'group_0'}, dimensions={0}, use_global_device_ids=true | all-gather | bytes 2560 | tf_op jit(solution)/shard_map/all_gather | solution.py:22
  29.4 0.8 copy.27
  30.2 0.2 fusion.2
  30.5 0.9 select_reduce_fusion
  31.5 0.7 broadcast_multiply_fusion.1
  32.1 1.4 scatter_custom_fusion
  33.5 0.7 all_to_all.9
  34.3 8.1 %all-to-all-start = ((s32[128,1,4]{2,1,0:T(1,128)}), s32[128,1,4]{2,1,0:T(1,128)S(1)}, u32[]{:S(2)}, u32[]{:S(2)}) async-start(s32[128,1,4]{2,1,0:T(1,128)} %bitcast.15), calls=%async_computation | async-start | bytes 131072 | tf_op jit(solution)/shard_map/all_to_all | solution.py:70
  42.4 0.7 neg.11
  43.0 1.5 divide_add_fusion
  44.5 6.2 %multiply_reduce_fusion = (f32[32768]{0:T(1024)S(1)}, f32[40,32768]{1,0:T(8,128)S(1)}) fusion(f32[40]{0:T(128)} %param.15, f32[32768]{0:T(1024)S(1)} %bitcast.62, f32[40]{0:T(128)} %param.14, f32[32768]{0:T(1024)S(1)} %bitcast.61, f32[40]{0:T(128)S(1)} %neg.11, f32[41,32768]{1,0:T(8,128)} %param.8, f32[40]{0:T(128)} %param.12, f32[40]{0:T(128)} %param.11), kind=kLoop, calls=%fused_computation.6 | loop fusion | flops 17006592 | bytes 10879776 | tf_op jit(solution)/shard_map/reduce_sum | solution.py:38
  50.8 1.4 slice_subtract_fusion
  52.1 0.5 pad_maximum_fusion
  52.6 1.1 copy.36
  53.7 0.6 slice.109
  54.3 5.9 %copy.32 = f32[41,256,128]{2,0,1:T(8,128)} copy(f32[41,256,128]{2,1,0:T(8,128)S(1)} %slice.109) | data formatting | bytes 10747904 | tf_op jit(solution)/shard_map/reshape | solution.py:69
  60.2 0.2 maximum_reduce_fusion
  60.7 0.1 copy.31
  60.9 8.7 %gather_fusion = f32[512,41,128]{2,1,0:T(8,128)} fusion(f32[41,256,128]{2,0,1:T(8,128)} %copy.32, s32[1024]{0:T(1024)S(1)} %pad_clamp_fusion), kind=kCustom, calls=%fused_computation | custom fusion | bytes 21497856 | tf_op jit(solution)/shard_map/jit(_take)/gather | solution.py:72
  69.6 13.3 %copy_select_fusion = f32[41,128,4,128]{3,2,0,1:T(4,128)} fusion(f32[41,128,4,128]{3,0,2,1:T(8,128)} %bitcast.57, pred[128,4]{1,0:T(8,128)(4,1)S(1)} %copy.31), kind=kLoop, calls=%fused_computation.4 | loop fusion | flops 2686976 | bytes 21496320 | tf_op jit(solution)/shard_map/jit(_take)/select_n | solution.py:72
  83.0 10.3 %all-to-all-start.1 = ((f32[41,128,4,128]{3,2,0,1:T(4,128)}), f32[41,128,4,128]{3,2,0,1:T(4,128)}, u32[]{:S(2)}, u32[]{:S(2)}) async-start(f32[41,128,4,128]{3,2,0,1:T(4,128)} %copy_select_fusion), calls=%async_computation.1 | async-start | bytes 21495808 | tf_op jit(solution)/shard_map/all_to_all | solution.py:73
  93.2 0.1 compare_and_fusion
  93.4 0.1 compare_select_fusion
  93.5 139.9 %all-to-all-done.1 = f32[41,128,4,128]{3,2,0,1:T(4,128)} async-done(((f32[41,128,4,128]{3,2,0,1:T(4,128)}), f32[41,128,4,128]{3,2,0,1:T(4,128)}, u32[]{:S(2)}, u32[]{:S(2)}) %all-to-all-start.1) | async-done | bytes 10747936 | tf_op jit(solution)/shard_map/all_to_all | solution.py:73
  233.4 21.9 %copy.34 = f32[41,128,4,128]{0,3,2,1:T(8,128)} copy(f32[41,128,4,128]{3,2,0,1:T(4,128)} %all-to-all-done.1) | data formatting | bytes 21495808 | tf_op jit(solution)/shard_map/all_to_all | solution.py:73
  255.4 118.8 %gather_fusion.1 = f32[32768,41]{1,0:T(8,128)} fusion(f32[41,65536]{0,1:T(8,128)} %bitcast.56, s32[32768]{0:T(1024)S(1)} %broadcast_clamp_fusion), kind=kCustom, calls=%fused_computation.1 | custom fusion | bytes 10878976 | tf_op jit(solution)/shard_map/jit(_take)/gather | solution.py:81
  374.2 19.1 %select_bitcast_fusion = f32[41,32768]{0,1:T(8,128)} fusion(f32[32768,41]{1,0:T(8,128)} %gather_fusion.1, pred[32768]{0:T(1024)(128)(4,1)S(1)} %get-tuple-element.7), kind=kLoop, calls=%fused_computation.3 | loop fusion | flops 1343488 | bytes 10780672 | tf_op jit(solution)/shard_map/jit(_take)/select_n | solution.py:81
  393.3 12.1 %copy.35 = f32[41,32768]{1,0:T(8,128)} copy(f32[41,32768]{0,1:T(8,128)} %select_bitcast_fusion) | data formatting | bytes 10747904 | tf_op jit(solution)/shard_map/jit(_take)/select_n | solution.py:81
  (19 shorter events, 0.5 us)
Async XLA Ops:
  34.3 25.9 %all-to-all-start = ((s32[128,1,4]{2,1,0:T(1,128)}), s32[128,1,4]{2,1,0:T(1,128)S(1)}, u32[]{:S(2)}, u32[]{:S(2)}) async-start(s32[128,1,4]{2,1,0:T(1,128)} %bitcast.15), calls=%async_computation | async-start | bytes 131072 | tf_op jit(solution)/shard_map/all_to_all | solution.py:70
  83.0 10.3 %copy-start = (s32[256,128]{1,0:T(8,128)S(1)}, s32[256,128]{1,0:T(8,128)}, u32[]{:S(2)}) copy-start(s32[256,128]{1,0:T(8,128)} %param.10) | copy-start | bytes 393220
  83.0 150.5 %all-to-all-start.1 = ((f32[41,128,4,128]{3,2,0,1:T(4,128)}), f32[41,128,4,128]{3,2,0,1:T(4,128)}, u32[]{:S(2)}, u32[]{:S(2)}) async-start(f32[41,128,4,128]{3,2,0,1:T(4,128)} %copy_select_fusion), calls=%async_computation.1 | async-start | bytes 21495808 | tf_op jit(solution)/shard_map/all_to_all | solution.py:73
where the time goes:
time: 413 us; the launch traced here: 405 us
  local copies, waits for them, and re-layouts  172 us (42%)
  waiting for transfers between devices  140 us (34%)
  other arithmetic  45.9 us (11%)
  blocking collectives  28.6 us (7%)
  starting transfers between devices  18.4 us (4%)
    all_to_all x1, waiting for transfers between devices, on_device(): lax.all_to_all(served.reshape(width, wanted.shape[0], wanted.shape[1], ti...  140 us
    gather x1, local copies, waits for them, and re-layouts, on_device(): jnp.take(arrived.reshape(width, devices * capacity * tile_width), flat_co...  119 us
    all_gather x4, blocking collectives, prefix_by_axis(): pieces = lax.all_gather(subtotal, axis)  28.6 us
    all_to_all x1, local copies, waits for them, and re-layouts, on_device(): lax.all_to_all(served.reshape(width, wanted.shape[0], wanted.shape[1], ti...  21.9 us
    select_n x2, other arithmetic, on_device(): jnp.take(arrived.reshape(width, devices * capacity * tile_width), flat_co...  19.2 us
    select_n x1, other arithmetic, on_device(): served = jnp.take(advanced, picked, axis=1)  13.3 us
    select_n x1, local copies, waits for them, and re-layouts, on_device(): jnp.take(arrived.reshape(width, devices * capacity * tile_width), flat_co...  12.1 us
    all_to_all x1, starting transfers between devices, on_device(): lax.all_to_all(served.reshape(width, wanted.shape[0], wanted.shape[1], ti...  10.3 us
  transfers between devices with their start and end apart: 2, of which 1 were waited for; matrix products, arithmetic and copies ran while one was open for 4% of the time, Pallas kernels for 0%

commit v1 on v0

v1 whole, which is shorter than its diff:
```python
import functools

import jax
import jax.numpy as jnp
from jax import lax
from jax.experimental import pallas as pl
from jax.experimental.pallas import tpu as pltpu
from jax.sharding import PartitionSpec as P

AXES = ("group", "peer")
DEVICES = 128
BLOCKS = 256
LANES = 128
ROWS = 41
CAP = 4
TIME_STEP = 0.25


def advance(block, half_volt, steepness, gate_rate, conductance, reversal):
    voltage = block[0:1, :]
    steady = jax.nn.sigmoid((voltage - half_volt) * steepness)
    damping = jnp.exp(-gate_rate * (1.0 + jax.nn.sigmoid(voltage)))
    gates = steady + (block - steady) * damping
    current = jnp.sum(conductance * gates * (voltage - reversal), axis=0, keepdims=True)
    row = lax.broadcasted_iota(jnp.int32, block.shape, 0)
    return jnp.where(row == 0, voltage - TIME_STEP * current, gates)


def pack_kernel(per_step, starts_ref, states_ref, hv, st, gr, co, re, out_ref):
    step = pl.program_id(0)
    params = [r[...] for r in (hv, st, gr, co, re)]
    for j in range(per_step):
        first = starts_ref[step * per_step + j]
        for k in range(CAP):
            at = jnp.minimum(first + k, BLOCKS - 1)
            block = states_ref[:, pl.ds(pl.multiple_of(at * LANES, LANES), LANES)]
            out_ref[j, k * ROWS:(k + 1) * ROWS, :] = advance(block, *params)


def place_kernel(per_step, slots_ref, arrived_ref, perm_ref, out_ref):
    step = pl.program_id(0)
    for j in range(per_step):
        slot = slots_ref[step * per_step + j]
        part, rank = slot // CAP, slot % CAP
        block = arrived_ref[part, pl.ds(rank * ROWS, ROWS), :]
        index = jnp.broadcast_to(perm_ref[j:j + 1, :], (ROWS, LANES))
        out_ref[:, j * LANES:(j + 1) * LANES] = jnp.take_along_axis(block, index, axis=1)


def row_params(values, dummy):
    padded = jnp.concatenate([jnp.full((1,), dummy, values.dtype), values])
    return jnp.broadcast_to(padded[:, None], (ROWS, LANES))


def on_device(states, block_part, tile_perm, half_volt, steepness, gate_rate, conductance, reversal):
    me = lax.axis_index(AXES)
    parts = jnp.arange(DEVICES, dtype=jnp.int32)
    onehot = (block_part[:, None] == parts[None, :]).astype(jnp.float32)
    order = jnp.arange(BLOCKS, dtype=jnp.int32)
    lower = (order[:, None] > order[None, :]).astype(jnp.float32)
    before = lax.dot(lower, onehot)
    rank = jnp.sum(onehot * before, axis=1).astype(jnp.int32)
    slots = block_part * CAP + rank
    counts = jnp.sum(onehot, axis=0).astype(jnp.int32)
    every = lax.all_gather(counts, AXES)
    mine = jnp.sum(jnp.where(parts[None, :] == me, every, 0), axis=1).astype(jnp.float32)
    starts = lax.dot((parts[:, None] > parts[None, :]).astype(jnp.float32), mine).astype(jnp.int32)

    params = [
        row_params(half_volt, 0.0),
        row_params(steepness, 1.0),
        row_params(gate_rate, 1.0),
        row_params(conductance, 0.0),
        row_params(reversal, 0.0),
    ]
    whole = pl.BlockSpec(memory_space=pltpu.VMEM)
    smem = pl.BlockSpec(memory_space=pltpu.SMEM)
    per = 8
    served = pl.pallas_call(
        functools.partial(pack_kernel, per),
        grid=(DEVICES // per,),
        out_shape=jax.ShapeDtypeStruct((DEVICES, CAP * ROWS, LANES), jnp.float32),
        in_specs=[smem, whole] + [whole] * 5,
        out_specs=pl.BlockSpec((per, CAP * ROWS, LANES), lambda i: (i, 0, 0)),
        compiler_params=pltpu.CompilerParams(vmem_limit_bytes=32 * 1024 * 1024),
    )(starts, states, *params)
    arrived = lax.all_to_all(served, AXES, split_axis=0, concat_axis=0, tiled=True)
    per = 16
    return pl.pallas_call(
        functools.partial(place_kernel, per),
        grid=(BLOCKS // per,),
        out_shape=jax.ShapeDtypeStruct((ROWS, BLOCKS * LANES), jnp.float32),
        in_specs=[smem, whole, pl.BlockSpec((per, LANES), lambda i: (i, 0))],
        out_specs=pl.BlockSpec((ROWS, per * LANES), lambda i: (0, i)),
        compiler_params=pltpu.CompilerParams(vmem_limit_bytes=32 * 1024 * 1024),
    )(slots, arrived, tile_perm)


def solution(mesh):
    split = P(None, AXES)
    placed = (split, P(AXES), P(AXES, None), P(), P(), P(), P(), P())
    return jax.shard_map(on_device, mesh=mesh, in_specs=placed, out_specs=split, check_vma=False)
```

time: 413 us -> 234 us (0.57); the launches traced: 405 us -> 234 us
  local copies, waits for them, and re-layouts: 172 us -> 7.19 us
  other arithmetic: 45.9 us -> 3.15 us
  Pallas kernels: 0 us -> 20.7 us
  blocking collectives: 28.6 us -> 46.7 us
  starting transfers between devices: 18.4 us -> 7.99 us
  waiting for transfers between devices: 140 us -> 148 us
    gather x2 -> x0, local copies, waits for them, and re-layouts: 128 us -> none  [the longest x1 119 us: on_device(): jnp.take(arrived.reshape(width, devices * capacity * tile_width), flat_co...]
    select_n x3 -> x0, other arithmetic: 32.6 us -> none  [the longest x2 19.2 us: on_device(): jnp.take(arrived.reshape(width, devices * capacity * tile_width), flat_co...]
    all_to_all x2 -> x0, local copies, waits for them, and re-layouts: 22.7 us -> none  [the longest x1 21.9 us: on_device(): lax.all_to_all(served.reshape(width, wanted.shape[0], wanted.shape[1], ti...]
    pallas_call x0 -> x2, Pallas kernels: none -> 20.7 us  [the longest x1 12.2 us: on_device(): pl.pallas_call(functools.partial(place_kernel, per), grid=(BLOCKS // per,...]
    all_gather x4 -> x1, blocking collectives: 28.6 us -> 46.7 us  [on_device(): every = lax.all_gather(counts, AXES)]
    select_n x1 -> x0, local copies, waits for them, and re-layouts: 12.1 us -> none  [on_device(): jnp.take(arrived.reshape(width, devices * capacity * tile_width), flat_co...]
    all_to_all x2 -> x1, starting transfers between devices: 18.4 us -> 7.99 us  [on_device(): lax.all_to_all(served, AXES, split_axis=0, concat_axis=0, tiled=True)]
    all_to_all x2 -> x1, waiting for transfers between devices: 140 us -> 148 us  [on_device(): lax.all_to_all(served, AXES, split_axis=0, concat_axis=0, tiled=True)]
  transfers between devices with their start and end apart: 2 -> 1, of which waited for: 1 -> 1; matrix products, arithmetic and copies ran while one was open for 4% -> 0% of each run, Pallas kernels for 0% -> 0%
where the time goes in v1:
time: 234 us
  waiting for transfers between devices  148 us (63%)
  blocking collectives  46.7 us (20%)
  Pallas kernels  20.7 us (9%)
  starting transfers between devices  7.99 us (3%)
  local copies, waits for them, and re-layouts  7.19 us (3%)
  other arithmetic  3.15 us (1%)
    all_to_all x1, waiting for transfers between devices, on_device(): lax.all_to_all(served, AXES, split_axis=0, concat_axis=0, tiled=True)  148 us
    all_gather x1, blocking collectives, on_device(): every = lax.all_gather(counts, AXES)  46.7 us
    pallas_call x1, Pallas kernels, on_device(): pl.pallas_call(functools.partial(place_kernel, per), grid=(BLOCKS // per,...  12.2 us
    pallas_call x1, Pallas kernels, on_device(): pl.pallas_call(functools.partial(pack_kernel, per), grid=(DEVICES // per,...  8.54 us
    all_to_all x1, starting transfers between devices, on_device(): lax.all_to_all(served, AXES, split_axis=0, concat_axis=0, tiled=True)  7.99 us
    unnamed x8, local copies, waits for them, and re-layouts  6.84 us
  transfers between devices with their start and end apart: 1, of which 1 were waited for; matrix products, arithmetic and copies ran while one was open for 0% of the time, Pallas kernels for 0%

profile of v1, /device:TPU:5, one launch (start us, length us, event | category | flops | bytes accessed | tf_op | source)
XLA Modules:
  0.0 234.0 jit_solution(12535949372717989941)
XLA Ops:
  0.0 0.8 convert_reduce_fusion
  0.8 46.7 %all-gather.1 = s32[128,1,128]{2,1,0:T(1,128)S(1)} all-gather(s32[1,1,128]{2,1,0:T(1,128)S(1)} %convert_bitcast_fusion), channel_id=2, replica_groups=mesh['group'=8,'peer'=16] {'group','peer'}, dimensions={0}, use_global_device_ids=true | all-gather | bytes 66048 | tf_op jit(solution)/shard_map/all_gather | solution.py:65
  47.5 0.1 select_reduce_fusion
  47.6 0.1 fusion.1.starts_ref
  47.7 0.8 pad_maximum_fusion.2
  48.5 0.7 pad_maximum_fusion
  49.2 0.7 pad_maximum_fusion.3
  50.0 0.1 broadcast_in_dim.25.st
  50.1 0.1 broadcast_in_dim.26.gr
  50.1 0.1 broadcast_in_dim.27.co
  50.2 0.1 broadcast_in_dim.28.re
  50.3 0.1 broadcast_in_dim.24.hv
  50.3 0.0 copy-start.1
  50.4 2.8 %copy-done.1 = f32[41,32768]{1,0:T(8,128)S(1)} copy-done((f32[41,32768]{1,0:T(8,128)S(1)}, f32[41,32768]{1,0:T(8,128)}, u32[]{:S(2)}) %copy-start.1) | copy-done | bytes 5373976
  53.2 8.5 %shard_map.82 = f32[128,164,128]{2,1,0:T(8,128)S(1)} custom-call(s32[128]{0:T(128)S(1)} %fusion.1.starts_ref, f32[41,32768]{1,0:T(8,128)S(1)} %copy-done.1, f32[41,128]{1,0:T(8,128)S(1)} %broadcast_in_dim.24.hv, f32[41,128]{1,0:T(8,128)S(1)} %broadcast_in_dim.25.st, f32[41,128]{1,0:T(8,128)S(1)} %broadcast_in_dim.26.gr, f32[41,128]{1,0:T(8,128)S(1)} %broadcast_in_dim.27.co, ...), custom_call_target="tpu_custom_call" | custom-call | tf_op jit(solution)/shard_map/pallas_call | solution.py:79
  61.7 0.0 copy-start
  61.7 4.0 %copy-done = f32[128,164,128]{2,1,0:T(8,128)} copy-done((f32[128,164,128]{2,1,0:T(8,128)}, f32[128,164,128]{2,1,0:T(8,128)S(1)}, u32[]{:S(2)}) %copy-start) | copy-done | bytes 10747928
  65.7 0.0 copy-start.3
  65.7 0.0 copy-start.2
  65.7 8.0 %all-to-all-start = ((f32[128,164,128]{2,1,0:T(8,128)}), f32[128,164,128]{2,1,0:T(8,128)}, u32[]{:S(2)}, u32[]{:S(2)}) async-start(f32[128,164,128]{2,1,0:T(8,128)} %copy-done), calls=%async_computation | async-start | bytes 22020096 | tf_op jit(solution)/shard_map/all_to_all | solution.py:87
  73.7 0.0 copy-done.3
  73.7 0.2 fusion
  74.0 147.8 %all-to-all-done.arrived_ref = f32[128,164,128]{2,1,0:T(8,128)} async-done(((f32[128,164,128]{2,1,0:T(8,128)}), f32[128,164,128]{2,1,0:T(8,128)}, u32[]{:S(2)}, u32[]{:S(2)}) %all-to-all-start) | async-done | bytes 10747936 | tf_op jit(solution)/shard_map/all_to_all | solution.py:87
  221.8 0.0 copy-done.2
  221.8 12.2 %shard_map.83 = f32[41,32768]{1,0:T(8,128)} custom-call(s32[256]{0:T(256)S(1)} %convert_add_fusion.slots_ref, f32[128,164,128]{2,1,0:T(8,128)} %all-to-all-done.arrived_ref, s32[256,128]{1,0:T(8,128)S(1)} %copy-done.2), custom_call_target="tpu_custom_call" | custom-call | tf_op jit(solution)/shard_map/pallas_call | solution.py:89
  (3 shorter events, 0.0 us)
Async XLA Ops:
  50.3 2.8 %copy-start.1 = (f32[41,32768]{1,0:T(8,128)S(1)}, f32[41,32768]{1,0:T(8,128)}, u32[]{:S(2)}) copy-start(f32[41,32768]{1,0:T(8,128)} %states_ref.1) | copy-start | bytes 16121860
  61.7 4.0 %copy-start = (f32[128,164,128]{2,1,0:T(8,128)}, f32[128,164,128]{2,1,0:T(8,128)S(1)}, u32[]{:S(2)}) copy-start(f32[128,164,128]{2,1,0:T(8,128)S(1)} %shard_map.82) | copy-start | bytes 32243716
  65.7 8.0 %copy-start.3 = (s32[256]{0:T(256)S(1)}, s32[256]{0:T(256)}, u32[]{:S(2)}) copy-start(s32[256]{0:T(256)} %param.9) | copy-start | bytes 3076
  65.7 156.0 %copy-start.2 = (s32[256,128]{1,0:T(8,128)S(1)}, s32[256,128]{1,0:T(8,128)}, u32[]{:S(2)}) copy-start(s32[256,128]{1,0:T(8,128)} %perm_ref.1) | copy-start | bytes 393220
  65.7 156.0 %all-to-all-start = ((f32[128,164,128]{2,1,0:T(8,128)}), f32[128,164,128]{2,1,0:T(8,128)}, u32[]{:S(2)}, u32[]{:S(2)}) async-start(f32[128,164,128]{2,1,0:T(8,128)} %copy-done), calls=%async_computation | async-start | bytes 22020096 | tf_op jit(solution)/shard_map/all_to_all | solution.py:87

commit v2 on v1

v2 whole, which is shorter than its diff:
```python
import functools

import jax
import jax.numpy as jnp
from jax import lax
from jax.experimental import pallas as pl
from jax.experimental.pallas import tpu as pltpu
from jax.sharding import PartitionSpec as P

AXES = ("group", "peer")
DEVICES = 128
BLOCKS = 256
LANES = 128
ROWS = 41
SLOTS = 4
TIME_STEP = 0.25
PIECE = 7
LIMIT = 176
SIZES = (4, 2, 4, 4)
STRIDES = (32, 16, 4, 1)
CORE = 1
ORDERS = ((3, 0, 2), (0, 2, 3), (2, 3, 0))
MESH = pl.DeviceIdType.MESH


def digits_of(device):
    return tuple(lax.rem(lax.div(device, st), sz) for st, sz in zip(STRIDES, SIZES))


def take_digits(number, dims):
    out = {}
    for d in reversed(dims):
        out[d] = lax.rem(number, SIZES[d])
        number = lax.div(number, SIZES[d])
    return out, number


def cells(stage, order, own, r):
    if stage == 3:
        fixed_s, free_p, list_dim, held_by = tuple(order), (0, 1, 2, 3), CORE, order[2]
    else:
        fixed_s = tuple(order[:stage])
        free_p = tuple(sorted(fixed_s + (CORE,)))
        list_dim = order[stage]
        held_by = CORE if stage == 0 else order[stage - 1]
    free_s = tuple(d for d in range(4) if d not in fixed_s and d != list_dim)
    s, rest = take_digits(r, free_s)
    p, rest = take_digits(rest, free_p)
    s[list_dim] = rest
    slab = sum((s[d] if d in s else own[d]) * STRIDES[d] for d in range(4))
    part = sum((p[d] if d in p else own[d]) * STRIDES[d] for d in range(4))
    return slab, part, p[held_by]


def index_lists(stage, order, own, counts, cap):
    lists = 2 if stage == 3 else 4
    size = 256 // lists
    col = lax.broadcasted_iota(jnp.int32, (256, 1), 0)
    row = lax.broadcasted_iota(jnp.int32, (1, 256), 1)
    slab, part, held = cells(stage, order, own, col)
    slab_r, part_r, held_r = cells(stage, order, own, row)
    device = lax.broadcasted_iota(jnp.int32, (1, DEVICES), 1)
    pick = (part == device).astype(jnp.float32)
    by_part = lax.dot_general(pick, counts, (((1,), (1,)), ((), ())))
    n = jnp.sum(jnp.where(slab == device, by_part, 0.0), axis=1, keepdims=True)
    earlier = (held_r == held) & (part_r * DEVICES + slab_r < part * DEVICES + slab)
    base = lax.dot(earlier.astype(jnp.float32), n).astype(jnp.int32)
    base = base + held * (BLOCKS if stage == 0 else cap)
    same = lax.div(row, size) == lax.div(col, size)
    place = lax.dot((same & (row < col)).astype(jnp.float32), n).astype(jnp.int32)
    n = n.astype(jnp.int32)
    out = []
    j = lax.broadcasted_iota(jnp.int32, (1, 256), 1)
    for k in range(lists):
        part_of = slice(k * size, (k + 1) * size)
        lo, shift, width = place[part_of], (base - place)[part_of], n[part_of]
        inside = (j >= lo) & (j < lo + width)
        out.append(j + jnp.sum(jnp.where(inside, shift, 0), axis=0, keepdims=True))
    return jnp.concatenate(out, axis=0)


def longest_list(counts):
    grid = counts.reshape(SIZES + SIZES)
    longest = []
    for order in ORDERS:
        for stage in range(3):
            done, to = order[:stage], order[:stage + 1]
            keep = set(d for d in (0, 2, 3) if d not in done)
            axes = tuple(d for d in range(4) if d not in to) + tuple(4 + d for d in range(4) if d not in keep)
            longest.append(jnp.max(jnp.sum(grid, axis=axes)))
    return functools.reduce(jnp.maximum, longest)


def advance(block, half_volt, steepness, gate_rate, conductance, reversal):
    voltage = block[0:1, :]
    steady = jax.nn.sigmoid((voltage - half_volt) * steepness)
    damping = jnp.exp(-gate_rate * (1.0 + jax.nn.sigmoid(voltage)))
    gates = steady + (block - steady) * damping
    current = jnp.sum(conductance * gates * (voltage - reversal), axis=0, keepdims=True)
    row = lax.broadcasted_iota(jnp.int32, block.shape, 0)
    return jnp.where(row == 0, voltage - TIME_STEP * current, gates)


def move_kernel(cap, lists_ref, states_ref, hv, st, gr, co, re, out_ref, *scratch):
    adv, recv, stage, send = scratch[:3], (scratch[3:6], scratch[6:9], scratch[9:12]), scratch[12], scratch[13]
    swap_send, swap_recv, send_sem, recv_sem, last_send, last_recv = scratch[14:]
    me = lax.axis_index("group") * 16 + lax.axis_index("peer")
    own = digits_of(me)
    core = own[CORE]

    def at(coords):
        return (coords[0] * 2 + coords[CORE], coords[2] * 4 + coords[3])

    partner = at((own[0], 1 - core, own[2], own[3]))
    params = [r[...] for r in (hv, st, gr, co, re)]
    half = 3 * PIECE
    mine_at = core * (BLOCKS * PIECE)

    def update(i, carry):
        for u in range(8):
            b = i * 8 + u
            new = advance(states_ref[:, pl.ds(pl.multiple_of(b * LANES, LANES), LANES)], *params)
            low = new[0:half]
            high = jnp.concatenate([new[half:ROWS], new[ROWS - 1:ROWS]], axis=0)
            keep = jnp.where(core == 0, low, high)
            give = jnp.where(core == 0, high, low)
            for t in range(3):
                adv[t][pl.ds(mine_at + b * PIECE, PIECE), :] = keep[t * PIECE:(t + 1) * PIECE]
                stage[t, pl.ds(b * PIECE, PIECE), :] = give[t * PIECE:(t + 1) * PIECE]
        return carry

    lax.fori_loop(0, BLOCKS // 8, update, 0)

    def swap(t):
        return pltpu.make_async_remote_copy(
            src_ref=stage.at[t],
            dst_ref=adv[t].at[pl.ds(pl.multiple_of(mine_at, 8), BLOCKS * PIECE)],
            send_sem=swap_send.at[t], recv_sem=swap_recv.at[t], device_id=partner, device_id_type=MESH)

    for t in range(3):
        swap(t).start()

    def hop(t, ph, delta):
        dim = ORDERS[t][ph]
        to = lax.rem(own[dim] + delta, 4)
        coords = tuple(to if d == dim else own[d] for d in range(4))
        return pltpu.make_async_remote_copy(
            src_ref=send.at[t, delta - 1],
            dst_ref=recv[ph][t].at[pl.ds(pl.multiple_of(own[dim] * (cap * PIECE), 8), cap * PIECE)],
            send_sem=send_sem.at[ph, t, delta - 1], recv_sem=recv_sem.at[ph, t, delta - 1],
            device_id=at(coords), device_id_type=MESH)

    def gather(source, target, start, row, count):
        def body(i, carry):
            for u in range(8):
                j = i * 8 + u
                target[pl.ds(start + j * PIECE, PIECE), :] = source[pl.ds(lists_ref[row, j] * PIECE, PIECE), :]
            return carry

        lax.fori_loop(0, count // 8, body, 0)

    for ph in range(3):
        for t in range(3):
            dim = ORDERS[t][ph]
            if ph == 0:
                swap(t).wait()
                source = adv[t]
            else:
                for delta in (2, 1, 3):
                    hop(t, ph - 1, delta).wait()
                source = recv[ph - 1][t]
            for delta in (2, 1, 3, 0):
                to = lax.rem(own[dim] + delta, 4)
                row = (ph * 3 + t) * 4 + to
                if delta:
                    gather(source, send.at[t, delta - 1], 0, row, cap)
                    hop(t, ph, delta).start()
                else:
                    gather(source, recv[ph][t], own[dim] * (cap * PIECE), row, cap)

    def last(t):
        return pltpu.make_async_remote_copy(
            src_ref=stage.at[t], dst_ref=out_ref.at[core, t],
            send_sem=last_send.at[t], recv_sem=last_recv.at[t], device_id=partner, device_id_type=MESH)

    for t in range(3):
        for delta in (2, 1, 3):
            hop(t, 2, delta).wait()
        gather(recv[2][t], stage.at[t], 0, 36 + t * 2 + 1 - core, BLOCKS)
        last(t).start()
    for t in range(3):
        gather(recv[2][t], out_ref.at[core, t], 0, 36 + t * 2 + core, BLOCKS)
    for t in range(3):
        last(t).wait()


def settle_kernel(per_step, where_ref, parts_ref, perm_ref, out_ref):
    step = pl.program_id(0)
    for j in range(per_step):
        at = where_ref[step * per_step + j] * PIECE
        rows = [parts_ref[h, t, pl.ds(at, PIECE), :] for h in range(2) for t in range(3)]
        block = jnp.concatenate(rows, axis=0)[0:ROWS]
        index = jnp.broadcast_to(perm_ref[j:j + 1, :], (ROWS, LANES))
        out_ref[:, j * LANES:(j + 1) * LANES] = jnp.take_along_axis(block, index, axis=1)


def pack_kernel(per_step, starts_ref, states_ref, hv, st, gr, co, re, out_ref):
    step = pl.program_id(0)
    params = [r[...] for r in (hv, st, gr, co, re)]
    for j in range(per_step):
        first = starts_ref[step * per_step + j]
        for k in range(SLOTS):
            at = jnp.minimum(first + k, BLOCKS - 1)
            block = states_ref[:, pl.ds(pl.multiple_of(at * LANES, LANES), LANES)]
            out_ref[j, k * ROWS:(k + 1) * ROWS, :] = advance(block, *params)


def place_kernel(per_step, slots_ref, arrived_ref, perm_ref, out_ref):
    step = pl.program_id(0)
    for j in range(per_step):
        slot = slots_ref[step * per_step + j]
        part, rank = slot // SLOTS, slot % SLOTS
        block = arrived_ref[part, pl.ds(rank * ROWS, ROWS), :]
        index = jnp.broadcast_to(perm_ref[j:j + 1, :], (ROWS, LANES))
        out_ref[:, j * LANES:(j + 1) * LANES] = jnp.take_along_axis(block, index, axis=1)


def row_params(values, dummy):
    padded = jnp.concatenate([jnp.full((1,), dummy, values.dtype), values])
    return jnp.broadcast_to(padded[:, None], (ROWS, LANES))


WHOLE = pl.BlockSpec(memory_space=pltpu.VMEM)
SCALARS = pl.BlockSpec(memory_space=pltpu.SMEM)


def direct_route(counts, states, params, block_part, rank, tile_perm):
    me = lax.axis_index(AXES)
    parts = jnp.arange(DEVICES, dtype=jnp.int32)
    mine = jnp.sum(jnp.where(parts[None, :] == me, counts, 0.0), axis=1)
    starts = lax.dot((parts[:, None] > parts[None, :]).astype(jnp.float32), mine).astype(jnp.int32)
    per = 8
    served = pl.pallas_call(
        functools.partial(pack_kernel, per),
        grid=(DEVICES // per,),
        out_shape=jax.ShapeDtypeStruct((DEVICES, SLOTS * ROWS, LANES), jnp.float32),
        in_specs=[SCALARS, WHOLE] + [WHOLE] * 5,
        out_specs=pl.BlockSpec((per, SLOTS * ROWS, LANES), lambda i: (i, 0, 0)),
        compiler_params=pltpu.CompilerParams(vmem_limit_bytes=32 * 1024 * 1024),
    )(starts, states, *params)
    arrived = lax.all_to_all(served, AXES, split_axis=0, concat_axis=0, tiled=True)
    per = 16
    return pl.pallas_call(
        functools.partial(place_kernel, per),
        grid=(BLOCKS // per,),
        out_shape=jax.ShapeDtypeStruct((ROWS, BLOCKS * LANES), jnp.float32),
        in_specs=[SCALARS, WHOLE, pl.BlockSpec((per, LANES), lambda i: (i, 0))],
        out_specs=pl.BlockSpec((ROWS, per * LANES), lambda i: (0, i)),
        compiler_params=pltpu.CompilerParams(vmem_limit_bytes=32 * 1024 * 1024),
    )(block_part * SLOTS + rank, arrived, tile_perm)


def staged_route(cap, counts, states, params, block_part, rank, tile_perm):
    me = lax.axis_index("group") * 16 + lax.axis_index("peer")
    own = digits_of(me)
    lists = [index_lists(ph, ORDERS[t], own, counts, cap) for ph in range(3) for t in range(3)]
    lists += [index_lists(3, ORDERS[t], own, counts, cap) for t in range(3)]
    lists = jnp.concatenate(lists, axis=0)
    dma = pltpu.SemaphoreType.DMA
    parts = pl.pallas_call(
        functools.partial(move_kernel, cap),
        out_shape=jax.ShapeDtypeStruct((2, 3, BLOCKS * PIECE, LANES), jnp.float32),
        in_specs=[SCALARS, WHOLE] + [WHOLE] * 5,
        out_specs=WHOLE,
        scratch_shapes=[
            *[pltpu.VMEM((2 * BLOCKS * PIECE, LANES), jnp.float32)] * 3,
            *[pltpu.VMEM((4 * cap * PIECE, LANES), jnp.float32)] * 9,
            pltpu.VMEM((3, BLOCKS * PIECE, LANES), jnp.float32),
            pltpu.VMEM((3, 3, cap * PIECE, LANES), jnp.float32),
            dma((3,)), dma((3,)), dma((3, 3, 3)), dma((3, 3, 3)), dma((3,)), dma((3,)),
        ],
        compiler_params=pltpu.CompilerParams(has_side_effects=True, vmem_limit_bytes=60 * 1024 * 1024),
    )(lists, states, *params)
    number = jnp.arange(DEVICES, dtype=jnp.int32)
    ours = jnp.sum(jnp.where(number[:, None] == me, counts, 0.0), axis=0)
    ahead = lax.dot((number[:, None] > number[None, :]).astype(jnp.float32), ours)
    onehot = block_part[:, None] == number[None, :]
    where = jnp.sum(jnp.where(onehot, ahead[None, :], 0.0), axis=1).astype(jnp.int32) + rank
    per = 16
    return pl.pallas_call(
        functools.partial(settle_kernel, per),
        grid=(BLOCKS // per,),
        out_shape=jax.ShapeDtypeStruct((ROWS, BLOCKS * LANES), jnp.float32),
        in_specs=[SCALARS, WHOLE, pl.BlockSpec((per, LANES), lambda i: (i, 0))],
        out_specs=pl.BlockSpec((ROWS, per * LANES), lambda i: (0, i)),
        compiler_params=pltpu.CompilerParams(vmem_limit_bytes=32 * 1024 * 1024),
    )(where, parts, tile_perm)


def on_device(states, block_part, tile_perm, half_volt, steepness, gate_rate, conductance, reversal):
    parts = jnp.arange(DEVICES, dtype=jnp.int32)
    onehot = (block_part[:, None] == parts[None, :]).astype(jnp.float32)
    order = jnp.arange(BLOCKS, dtype=jnp.int32)
    before = lax.dot((order[:, None] > order[None, :]).astype(jnp.float32), onehot)
    rank = jnp.sum(onehot * before, axis=1).astype(jnp.int32)
    counts = jnp.sum(onehot, axis=0)
    counts = lax.all_gather(counts, "peer")
    counts = lax.all_gather(counts, "group").reshape(DEVICES, DEVICES)
    params = [
        row_params(half_volt, 0.0),
        row_params(steepness, 1.0),
        row_params(gate_rate, 1.0),
        row_params(conductance, 0.0),
        row_params(reversal, 0.0),
    ]
    fits = longest_list(counts) <= LIMIT
    args = (counts, states, params, block_part, rank, tile_perm)
    return lax.cond(fits, functools.partial(staged_route, LIMIT), direct_route, *args)


def solution(mesh):
    split = P(None, AXES)
    placed = (split, P(AXES), P(AXES, None), P(), P(), P(), P(), P())
    return jax.shard_map(on_device, mesh=mesh, in_specs=placed, out_specs=split, check_vma=False)
```

time: 234 us -> 210 us (0.90); the launches traced: 234 us -> 207 us
  waiting for transfers between devices: 148 us -> 0 us
  Pallas kernels: 20.7 us -> 127 us
  other arithmetic: 3.15 us -> 16.5 us
  blocking collectives: 46.7 us -> 34.8 us
  matrix products: 0.37 us -> 8.93 us
  starting transfers between devices: 7.99 us -> 0 us
  local copies, waits for them, and re-layouts: 7.19 us -> 13.3 us
  between operations: 0.07 us -> 6.01 us
    all_to_all x1 -> x0, waiting for transfers between devices: 148 us -> none  [on_device(): lax.all_to_all(served, AXES, split_axis=0, concat_axis=0, tiled=True)]
    pallas_call x2, Pallas kernels: 20.7 us -> 127 us  [the longest x1 122 us: staged_route(): pl.pallas_call(functools.partial(move_kernel, cap), out_shape=jax.ShapeDt...]
    all_gather x1 -> x2, blocking collectives: 46.7 us -> 34.8 us  [the longest x1 18.7 us: on_device(): counts = lax.all_gather(counts, 'group').reshape(DEVICES, DEVICES)]
    dot_general x2 -> x33, matrix products: 0.37 us -> 8.93 us  [the longest x12 3.06 us: index_lists(): base = lax.dot(earlier.astype(jnp.float32), n).astype(jnp.int32)]
    all_to_all x1 -> x0, starting transfers between devices: 7.99 us -> none  [on_device(): lax.all_to_all(served, AXES, split_axis=0, concat_axis=0, tiled=True)]
    reduce_sum x2 -> x46, other arithmetic: 0.89 us -> 7 us  [the longest x38 4.22 us: index_lists(): out.append(j + jnp.sum(jnp.where(inside, shift, 0), axis=0, keepdims=True))]
    reduce_max x0 -> x9, other arithmetic: none -> 5.65 us  [longest_list(): longest.append(jnp.max(jnp.sum(grid, axis=axes)))]
    unnamed x8 -> x6, local copies, waits for them, and re-layouts: 6.84 us -> 2.71 us
  transfers between devices with their start and end apart: 1 -> 0, of which waited for: 1 -> 0; matrix products, arithmetic and copies ran while one was open for 0% -> 0% of each run, Pallas kernels for 0% -> 0%
where the time goes in v2:
time: 210 us; the launch traced here: 207 us
  Pallas kernels  127 us (60%)
  blocking collectives  34.8 us (17%)
  other arithmetic  16.5 us (8%)
  local copies, waits for them, and re-layouts  13.3 us (6%)
  matrix products  8.93 us (4%)
  between operations  6.01 us (3%)
    pallas_call x1, Pallas kernels, staged_route(): pl.pallas_call(functools.partial(move_kernel, cap), out_shape=jax.ShapeDt...  122 us
    all_gather x1, blocking collectives, on_device(): counts = lax.all_gather(counts, 'group').reshape(DEVICES, DEVICES)  18.7 us
    all_gather x1, blocking collectives, on_device(): counts = lax.all_gather(counts, 'peer')  16.1 us
    reduce_max x9, other arithmetic, longest_list(): longest.append(jnp.max(jnp.sum(grid, axis=axes)))  5.65 us
    pallas_call x1, Pallas kernels, staged_route(): pl.pallas_call(functools.partial(settle_kernel, per), grid=(BLOCKS // per...  4.77 us
    reduce_sum x38, other arithmetic, index_lists(): out.append(j + jnp.sum(jnp.where(inside, shift, 0), axis=0, keepdims=True))  4.22 us

profile of v2, /device:TPU:5, one launch (start us, length us, event | category | flops | bytes accessed | tf_op | source)
XLA Modules:
  0.0 207.2 jit_solution(4404779433049698191)
XLA Ops:
  0.0 0.9 convert_reduce_fusion
  0.9 16.1 %all-gather.2 = f32[16,1,128]{2,1,0:T(1,128)S(1)} all-gather(f32[1,1,128]{2,1,0:T(1,128)S(1)} %bitcast.231), channel_id=2, replica_groups=mesh['group'=8,'peer'=16] {'peer'}, dimensions={0}, use_global_device_ids=true | all-gather | bytes 8704 | tf_op jit(solution)/shard_map/all_gather | solution.py:307
  17.0 18.7 %all-gather.1 = f32[128,128]{1,0:T(8,128)S(1)} all-gather(f32[16,128]{1,0:T(8,128)S(1)} %bitcast.134), channel_id=3, replica_groups=mesh['group'=8,'peer'=16] {'group'}, dimensions={0}, use_global_device_ids=true | all-gather | bytes 73728 | tf_op jit(solution)/shard_map/all_gather | solution.py:308
  35.7 2.7 %reshape_reshape.3 = f32[4,2,4,4,4,2,4,4]{7,6,5,4,3,2,1,0:T(4,128)S(1)} reshape(f32[128,128]{1,0:T(8,128)S(1)} %all-gather.1) | data formatting | bytes 131072 | tf_op jit(solution)/shard_map/reshape;reshape | solution.py:83
  38.4 1.5 fusion.189
  39.8 0.7 reduce_max.82
  40.5 0.3 reduce_sum.702
  41.1 0.6 reduce_max.81
  43.0 0.6 reduce_max.83
  44.6 0.6 reduce_max.84
  45.8 0.6 reduce_max.85
  47.1 0.6 reduce_max.86
  48.4 0.6 reduce_max.87
  49.7 0.6 reduce_max.88
  50.9 0.6 reduce_max.89
  52.2 0.8 pad_maximum_fusion.3
  53.1 0.8 pad_maximum_fusion
  54.0 0.7 pad_maximum_fusion.2
  54.8 1.0 fusion.187
  55.8 148.7 %conditional.1 = (f32[41,32768]{1,0:T(8,128)S(1)}) conditional(s32[]{:T(128)} %convert_element_type.267, (s32[256]{0:T(256)S(1)}, s32[256]{0:T(256)S(1)}, f32[128,128]{1,0:T(8,128)S(1)}, f32[41,32768]{1,0:T(8,128)}, f32[41,128]{1,0:T(8,128)S(1)}, /*index=5*/f32[41,128]{1,0:T(8,128)S(1)}, f32[41,128]{1,0:T(8,128)S(1)}, f32[41,128]{1,0:T(8,128)S(1)}, ...), branch_computations={%region_22.24_spmd, %region_24.79_spmd} | conditional | flops 87991328 | bytes 75829656 | solution.py:318
  59.4 0.3 fusion.7
  60.9 0.3 fusion.6
  61.5 0.3 fusion.16
  62.3 0.3 fusion.5
  64.4 0.3 fusion.14
  66.7 0.3 select_reduce_fusion.7
  68.8 0.3 fusion.12
  70.8 3.7 %concatenate.12.lists_ref = s32[42,256]{1,0:T(8,128)} concatenate(s32[1,256]{1,0:T(1,128)S(1)} %iota_add_fusion.41, s32[1,256]{1,0:T(1,128)S(1)} %iota_add_fusion.40, s32[1,256]{1,0:T(1,128)S(1)} %iota_add_fusion.39, s32[1,256]{1,0:T(1,128)S(1)} %iota_add_fusion.38, s32[1,256]{1,0:T(1,128)S(1)} %iota_add_fusion.37, s32[1,256]{1,0:T(1,128)S(1)} %iota_add_fusion.36, ...), dimensions={0} | concatenate | bytes 86016 | tf_op jit(solution)/shard_map/cond/branch_1_fun/concatenate | solution.py:268
  74.5 122.1 %branch_1_fun.2.parts_ref = f32[2,3,1792,128]{3,2,1,0:T(8,128)} custom-call(s32[42,256]{1,0:T(8,128)} %concatenate.12.lists_ref, f32[41,32768]{1,0:T(8,128)} %get-tuple-element.61.states_ref, f32[41,128]{1,0:T(8,128)S(1)} %get-tuple-element.62.hv, f32[41,128]{1,0:T(8,128)S(1)} %get-tuple-element.63.st, f32[41,128]{1,0:T(8,128)S(1)} %get-tuple-element.64.gr, ...), custom_call_target="tpu_custom_call" | custom-call | tf_op jit(solution)/shard_map/cond/branch_1_fun/pallas_call | solution.py:270
  197.0 2.6 %copy-done.1 = f32[2,3,1792,128]{3,2,1,0:T(8,128)S(1)} copy-done((f32[2,3,1792,128]{3,2,1,0:T(8,128)S(1)}, f32[2,3,1792,128]{3,2,1,0:T(8,128)}, u32[]{:S(2)}) %copy-start.1) | copy-done | bytes 5505048 | tf_op jit(solution)/shard_map/cond
  199.5 4.8 %branch_1_fun.3 = f32[41,32768]{1,0:T(8,128)S(1)} custom-call(s32[256]{0:T(256)S(1)} %convert_add_fusion.where_ref, f32[2,3,1792,128]{3,2,1,0:T(8,128)S(1)} %copy-done.1, s32[256,128]{1,0:T(8,128)S(1)} %get-tuple-element.67.perm_ref), custom_call_target="tpu_custom_call" | custom-call | tf_op jit(solution)/shard_map/cond/branch_1_fun/pallas_call | solution.py:290
  204.6 2.7 %copy-done.2 = f32[41,32768]{1,0:T(8,128)} copy-done((f32[41,32768]{1,0:T(8,128)}, f32[41,32768]{1,0:T(8,128)S(1)}, u32[]{:S(2)}) %copy-start.2) | copy-done | bytes 5373976
  (205 shorter events, 13.7 us)
Async XLA Ops:
  0.0 55.8 %copy-start.4 = (s32[256]{0:T(256)S(1)}, s32[256]{0:T(256)}, u32[]{:S(2)}) copy-start(s32[256]{0:T(256)} %param.11) | copy-start | bytes 3076
  0.0 55.8 %copy-start.3 = (s32[256,128]{1,0:T(8,128)S(1)}, s32[256,128]{1,0:T(8,128)}, u32[]{:S(2)}) copy-start(s32[256,128]{1,0:T(8,128)} %param.12) | copy-start | bytes 393220
  197.0 2.6 %copy-start.1 = (f32[2,3,1792,128]{3,2,1,0:T(8,128)S(1)}, f32[2,3,1792,128]{3,2,1,0:T(8,128)}, u32[]{:S(2)}) copy-start(f32[2,3,1792,128]{3,2,1,0:T(8,128)} %branch_1_fun.2.parts_ref) | copy-start | bytes 16515076 | tf_op jit(solution)/shard_map/cond
  204.5 2.7 %copy-start.2 = (f32[41,32768]{1,0:T(8,128)}, f32[41,32768]{1,0:T(8,128)S(1)}, u32[]{:S(2)}) copy-start(f32[41,32768]{1,0:T(8,128)S(1)} %get-tuple-element.239) | copy-start | bytes 16121860

commit v3 on v2

v3 whole, which is shorter than its diff:
```python
import functools

import jax
import jax.numpy as jnp
from jax import lax
from jax.experimental import pallas as pl
from jax.experimental.pallas import tpu as pltpu
from jax.sharding import PartitionSpec as P

AXES = ("group", "peer")
DEVICES = 128
BLOCKS = 256
LANES = 128
ROWS = 41
SLOTS = 4
TIME_STEP = 0.25
PIECE = 7
LIMIT = 176
SIZES = (4, 2, 4, 4)
STRIDES = (32, 16, 4, 1)
CORE = 1
ORDERS = ((3, 0, 2), (0, 2, 3), (2, 3, 0))
MESH = pl.DeviceIdType.MESH


def digits_of(device):
    return tuple(lax.rem(lax.div(device, st), n) for st, n in zip(STRIDES, SIZES))


def take_digits(number, dims):
    out = {}
    for d in reversed(dims):
        out[d] = number & (SIZES[d] - 1)
        number = number >> (SIZES[d].bit_length() - 1)
    return out, number


def cells(stage, order, own, r):
    if stage == 3:
        fixed_s, free_p, list_dim, held_by = tuple(order), (0, 1, 2, 3), CORE, order[2]
    else:
        fixed_s = tuple(order[:stage])
        free_p = tuple(sorted(fixed_s + (CORE,)))
        list_dim = order[stage]
        held_by = CORE if stage == 0 else order[stage - 1]
    free_s = tuple(d for d in range(4) if d not in fixed_s and d != list_dim)
    s, rest = take_digits(r, free_s)
    p, rest = take_digits(rest, free_p)
    s[list_dim] = rest
    slab = sum((s[d] if d in s else own[d]) * STRIDES[d] for d in range(4))
    part = sum((p[d] if d in p else own[d]) * STRIDES[d] for d in range(4))
    return slab, part, p[held_by]


def index_lists(stage, order, own, counts, cap):
    lists = 2 if stage == 3 else 4
    size = 256 // lists
    col = lax.broadcasted_iota(jnp.int32, (256, 1), 0)
    row = lax.broadcasted_iota(jnp.int32, (1, 256), 1)
    slab, part, held = cells(stage, order, own, col)
    slab_r, part_r, held_r = cells(stage, order, own, row)
    device = lax.broadcasted_iota(jnp.int32, (1, DEVICES), 1)
    pick = (part == device).astype(jnp.float32)
    by_part = lax.dot_general(pick, counts, (((1,), (1,)), ((), ())), preferred_element_type=jnp.float32)
    n = jnp.sum(jnp.where(slab == device, by_part, 0.0), axis=1, keepdims=True)
    wide = jnp.broadcast_to(n, (256, LANES))
    earlier = (held_r == held) & (part_r * DEVICES + slab_r < part * DEVICES + slab)
    base = jnp.dot(earlier.astype(jnp.float32), wide, preferred_element_type=jnp.float32)[:, 0:1].astype(jnp.int32)
    base = base + held * (BLOCKS if stage == 0 else cap)
    shift = size.bit_length() - 1
    ahead = ((row >> shift) == (col >> shift)) & (row < col)
    place = jnp.dot(ahead.astype(jnp.float32), wide, preferred_element_type=jnp.float32)[:, 0:1].astype(jnp.int32)
    end = place + n.astype(jnp.int32)
    gap = base - place
    limit = 2 * BLOCKS - 1 if stage == 0 else 4 * cap - 1
    out = []
    for k in range(lists):
        one = slice(k * size, (k + 1) * size)
        inside = (row >= place[one]) & (row < end[one])
        found = row + jnp.sum(jnp.where(inside, gap[one], 0), axis=0, keepdims=True)
        out.append(jnp.clip(found, 0, limit))
    return out


def same_key(dims):
    i = lax.broadcasted_iota(jnp.int32, (DEVICES, DEVICES), 0)
    j = lax.broadcasted_iota(jnp.int32, (DEVICES, DEVICES), 1)
    mask = sum((SIZES[d] - 1) * STRIDES[d] for d in dims)
    return ((i & mask) == (j & mask)).astype(jnp.float32)


def longest_list(counts):
    longest = None
    for order in ORDERS:
        for stage in range(3):
            to, left = order[:stage + 1], order[stage:]
            sums = jnp.dot(same_key(to), counts, preferred_element_type=jnp.float32)
            sums = jnp.dot(sums, same_key(left), preferred_element_type=jnp.float32)
            longest = sums if longest is None else jnp.maximum(longest, sums)
    return jnp.max(longest, axis=0, keepdims=True)


def advance(block, half_volt, steepness, gate_rate, conductance, reversal):
    voltage = block[0:1, :]
    steady = jax.nn.sigmoid((voltage - half_volt) * steepness)
    damping = jnp.exp(-gate_rate * (1.0 + jax.nn.sigmoid(voltage)))
    gates = steady + (block - steady) * damping
    current = jnp.sum(conductance * gates * (voltage - reversal), axis=0, keepdims=True)
    row = lax.broadcasted_iota(jnp.int32, block.shape, 0)
    return jnp.where(row == 0, voltage - TIME_STEP * current, gates)


def column(values):
    lane = lax.broadcasted_iota(jnp.int32, (ROWS, ROWS - 1), 1)
    row = lax.broadcasted_iota(jnp.int32, (ROWS, ROWS - 1), 0)
    picked = jnp.sum(jnp.where(lane == row - 1, values, 0.0), axis=1, keepdims=True)
    return jnp.broadcast_to(picked, (ROWS, LANES))


CHUNKS = 4
CHUNK = BLOCKS // CHUNKS


def move_kernel(cap, part_ref, states_ref, hv, st, gr, co, re, out_ref, where_ref, longest_ref, counts_ref, *scratch):
    adv, recv, stage, send = scratch[:3], (scratch[3:6], scratch[6:9], scratch[9:12]), scratch[12], scratch[13]
    states, tables, lists = scratch[14], scratch[15], scratch[16:28]
    (load_sem, table_sem, count_send, count_recv, swap_send, swap_recv, send_sem, recv_sem,
     last_send, last_recv) = scratch[28:]
    me = lax.axis_index("group") * 16 + lax.axis_index("peer")
    own = digits_of(me)
    core = own[CORE]

    def at(coords):
        return (coords[0] * 2 + coords[CORE], coords[2] * 4 + coords[3])

    def along(dim, delta):
        to = lax.rem(own[dim] + delta, SIZES[dim])
        return at(tuple(to if d == dim else own[d] for d in range(4)))

    def load(k):
        columns = pl.ds(k * CHUNK * LANES, CHUNK * LANES)
        return pltpu.make_async_copy(states_ref.at[:, columns], states.at[:, columns], load_sem.at[k])

    for k in range(CHUNKS):
        load(k).start()
    barrier = pltpu.get_barrier_semaphore()
    neighbours = [(d, delta) for d in range(4) for delta in range(1, SIZES[d])]
    for d, delta in neighbours:
        pl.semaphore_signal(barrier, inc=1, device_id=along(d, delta), device_id_type=MESH)

    parts = part_ref[...]
    onehot = (lax.broadcasted_iota(jnp.int32, (DEVICES, BLOCKS), 0) == parts).astype(jnp.float32)
    ones = jnp.ones((8, BLOCKS), jnp.float32)
    mine = lax.dot_general(ones, onehot, (((1,), (1,)), ((), ())), preferred_element_type=jnp.float32)[0:1]
    counts_ref[me] = mine
    params = [column(r[...]) for r in (hv, st, gr, co, re)]

    pl.semaphore_wait(barrier, len(neighbours))

    spread = (3, 2, 1, 0)

    def tell(k, delta):
        held = STRIDES[spread[k]]
        rows = pl.ds(lax.div(me, held) * held, held)
        return pltpu.make_async_remote_copy(
            src_ref=counts_ref.at[rows], dst_ref=counts_ref.at[rows],
            send_sem=count_send.at[k, delta - 1], recv_sem=count_recv.at[k, delta - 1],
            device_id=along(spread[k], delta), device_id_type=MESH)

    half = 3 * PIECE
    mine_at = core * (BLOCKS * PIECE)

    def update(i, carry):
        for u in range(8):
            b = i * 8 + u
            new = advance(states[:, pl.ds(pl.multiple_of(b * LANES, LANES), LANES)], *params)
            low = new[0:half]
            high = jnp.concatenate([new[half:ROWS], new[ROWS - 1:ROWS]], axis=0)
            keep = jnp.where(core == 0, low, high)
            give = jnp.where(core == 0, high, low)
            for t in range(3):
                adv[t][pl.ds(mine_at + b * PIECE, PIECE), :] = keep[t * PIECE:(t + 1) * PIECE]
                stage[t, pl.ds(b * PIECE, PIECE), :] = give[t * PIECE:(t + 1) * PIECE]
        return carry

    def swap(t, k):
        rows = CHUNK * PIECE
        return pltpu.make_async_remote_copy(
            src_ref=stage.at[t, pl.ds(k * rows, rows)],
            dst_ref=adv[t].at[pl.ds(pl.multiple_of(mine_at + k * rows, 8), rows)],
            send_sem=swap_send.at[t, k], recv_sem=swap_recv.at[t, k],
            device_id=along(CORE, 1), device_id_type=MESH)

    for k in range(CHUNKS):
        for delta in range(1, SIZES[spread[k]]):
            tell(k, delta).start()
        load(k).wait()
        lax.fori_loop(k * CHUNK // 8, (k + 1) * CHUNK // 8, update, 0)
        for t in range(3):
            swap(t, k).start()
        for delta in range(1, SIZES[spread[k]]):
            tell(k, delta).wait()

    counts = counts_ref[...].reshape(DEVICES, DEVICES)

    def table(ph, t):
        return pltpu.make_async_copy(tables.at[ph * 3 + t], lists[ph * 3 + t], table_sem.at[ph * 3 + t])

    def make_table(ph, t):
        found = index_lists(ph, ORDERS[t], own, counts, cap)
        for k, one in enumerate(found):
            tables[ph * 3 + t, k:k + 1, :] = one

    for t in range(3):
        make_table(0, t)
    for t in range(3):
        table(0, t).start()

    def hop(t, ph, delta):
        dim = ORDERS[t][ph]
        return pltpu.make_async_remote_copy(
            src_ref=send.at[t, delta - 1],
            dst_ref=recv[ph][t].at[pl.ds(pl.multiple_of(own[dim] * (cap * PIECE), 8), cap * PIECE)],
            send_sem=send_sem.at[ph, t, delta - 1], recv_sem=recv_sem.at[ph, t, delta - 1],
            device_id=along(dim, delta), device_id_type=MESH)

    def gather(source, target, start, which, row, count):
        def body(i, carry):
            for u in range(8):
                j = i * 8 + u
                target[pl.ds(start + j * PIECE, PIECE), :] = source[pl.ds(which[row, j] * PIECE, PIECE), :]
            return carry

        lax.fori_loop(0, count // 8, body, 0)

    for ph in range(3):
        for t in range(3):
            dim = ORDERS[t][ph]
            table(ph, t).wait()
            if ph == 0:
                for k in range(CHUNKS):
                    swap(t, k).wait()
                source = adv[t]
            else:
                for delta in (2, 1, 3):
                    hop(t, ph - 1, delta).wait()
                source = recv[ph - 1][t]
            for delta in (2, 1, 3, 0):
                to = lax.rem(own[dim] + delta, 4)
                if delta:
                    gather(source, send.at[t, delta - 1], 0, lists[ph * 3 + t], to, cap)
                    hop(t, ph, delta).start()
                else:
                    gather(source, recv[ph][t], own[dim] * (cap * PIECE), lists[ph * 3 + t], to, cap)
        for t in range(3):
            make_table(ph + 1, t)
        for t in range(3):
            table(ph + 1, t).start()
        if ph == 0:
            longest_ref[0, 0] = jnp.max(longest_list(counts)).astype(jnp.int32)
            r = lax.broadcasted_iota(jnp.int32, (BLOCKS, BLOCKS), 0)
            c = lax.broadcasted_iota(jnp.int32, (BLOCKS, BLOCKS), 1)
            before = jnp.dot(onehot, (r < c).astype(jnp.float32), preferred_element_type=jnp.float32)
            d = lax.broadcasted_iota(jnp.int32, (DEVICES, DEVICES), 0)
            e = lax.broadcasted_iota(jnp.int32, (DEVICES, DEVICES), 1)
            ahead = jnp.sum(jnp.where(e < d, mine, 0.0), axis=1, keepdims=True)
            where_ref[...] = jnp.sum(onehot * (before + ahead), axis=0, keepdims=True).astype(jnp.int32)

    def last(t):
        return pltpu.make_async_remote_copy(
            src_ref=stage.at[t], dst_ref=out_ref.at[core, t],
            send_sem=last_send.at[t], recv_sem=last_recv.at[t],
            device_id=along(CORE, 1), device_id_type=MESH)

    for t in range(3):
        table(3, t).wait()
        for delta in (2, 1, 3):
            hop(t, 2, delta).wait()
        gather(recv[2][t], stage.at[t], 0, lists[9 + t], 1 - core, BLOCKS)
        last(t).start()
    for t in range(3):
        gather(recv[2][t], out_ref.at[core, t], 0, lists[9 + t], core, BLOCKS)
    for t in range(3):
        last(t).wait()


def settle_kernel(per_step, where_ref, parts_ref, perm_ref, out_ref):
    step = pl.program_id(0)
    for j in range(per_step):
        at = where_ref[step * per_step + j] * PIECE
        rows = [parts_ref[h, t, pl.ds(at, PIECE), :] for h in range(2) for t in range(3)]
        block = jnp.concatenate(rows, axis=0)[0:ROWS]
        index = jnp.broadcast_to(perm_ref[j:j + 1, :], (ROWS, LANES))
        out_ref[:, j * LANES:(j + 1) * LANES] = jnp.take_along_axis(block, index, axis=1)


def pack_kernel(per_step, starts_ref, states_ref, hv, st, gr, co, re, out_ref):
    step = pl.program_id(0)
    params = [r[...] for r in (hv, st, gr, co, re)]
    for j in range(per_step):
        first = starts_ref[step * per_step + j]
        for k in range(SLOTS):
            at = jnp.minimum(first + k, BLOCKS - 1)
            block = states_ref[:, pl.ds(pl.multiple_of(at * LANES, LANES), LANES)]
            out_ref[j, k * ROWS:(k + 1) * ROWS, :] = advance(block, *params)


def place_kernel(per_step, slots_ref, arrived_ref, perm_ref, out_ref):
    step = pl.program_id(0)
    for j in range(per_step):
        slot = slots_ref[step * per_step + j]
        part, rank = slot // SLOTS, slot % SLOTS
        block = arrived_ref[part, pl.ds(rank * ROWS, ROWS), :]
        index = jnp.broadcast_to(perm_ref[j:j + 1, :], (ROWS, LANES))
        out_ref[:, j * LANES:(j + 1) * LANES] = jnp.take_along_axis(block, index, axis=1)


def row_params(values, dummy):
    padded = jnp.concatenate([jnp.full((1,), dummy, values.dtype), values])
    return jnp.broadcast_to(padded[:, None], (ROWS, LANES))


WHOLE = pl.BlockSpec(memory_space=pltpu.VMEM)
SCALARS = pl.BlockSpec(memory_space=pltpu.SMEM)


def direct_route(parts, where, counts, states, block_part, tile_perm, *values):
    me = lax.axis_index(AXES)
    number = jnp.arange(DEVICES, dtype=jnp.int32)
    onehot = (block_part[:, None] == number[None, :]).astype(jnp.float32)
    order = jnp.arange(BLOCKS, dtype=jnp.int32)
    before = lax.dot((order[:, None] > order[None, :]).astype(jnp.float32), onehot)
    rank = jnp.sum(onehot * before, axis=1).astype(jnp.int32)
    counts = counts.reshape(DEVICES, DEVICES)
    mine = jnp.sum(jnp.where(number[None, :] == me, counts, 0.0), axis=1)
    starts = lax.dot((number[:, None] > number[None, :]).astype(jnp.float32), mine).astype(jnp.int32)
    params = [row_params(v, d) for v, d in zip(values, (0.0, 1.0, 1.0, 0.0, 0.0))]
    per = 8
    served = pl.pallas_call(
        functools.partial(pack_kernel, per),
        grid=(DEVICES // per,),
        out_shape=jax.ShapeDtypeStruct((DEVICES, SLOTS * ROWS, LANES), jnp.float32),
        in_specs=[SCALARS, WHOLE] + [WHOLE] * 5,
        out_specs=pl.BlockSpec((per, SLOTS * ROWS, LANES), lambda i: (i, 0, 0)),
        compiler_params=pltpu.CompilerParams(vmem_limit_bytes=32 * 1024 * 1024),
    )(starts, states, *params)
    arrived = lax.all_to_all(served, AXES, split_axis=0, concat_axis=0, tiled=True)
    per = 16
    return pl.pallas_call(
        functools.partial(place_kernel, per),
        grid=(BLOCKS // per,),
        out_shape=jax.ShapeDtypeStruct((ROWS, BLOCKS * LANES), jnp.float32),
        in_specs=[SCALARS, WHOLE, pl.BlockSpec((per, LANES), lambda i: (i, 0))],
        out_specs=pl.BlockSpec((ROWS, per * LANES), lambda i: (0, i)),
        compiler_params=pltpu.CompilerParams(vmem_limit_bytes=32 * 1024 * 1024),
    )(block_part * SLOTS + rank, arrived, tile_perm)


def settle(parts, where, counts, states, block_part, tile_perm, *values):
    per = 16
    return pl.pallas_call(
        functools.partial(settle_kernel, per),
        grid=(BLOCKS // per,),
        out_shape=jax.ShapeDtypeStruct((ROWS, BLOCKS * LANES), jnp.float32),
        in_specs=[SCALARS, WHOLE, pl.BlockSpec((per, LANES), lambda i: (i, 0))],
        out_specs=pl.BlockSpec((ROWS, per * LANES), lambda i: (0, i)),
        compiler_params=pltpu.CompilerParams(vmem_limit_bytes=60 * 1024 * 1024),
    )(where, parts, tile_perm)


def on_device(states, block_part, tile_perm, *values):
    cap = LIMIT
    dma = pltpu.SemaphoreType.DMA
    parts, where, longest, counts = pl.pallas_call(
        functools.partial(move_kernel, cap),
        out_shape=(
            jax.ShapeDtypeStruct((2, 3, BLOCKS * PIECE, LANES), jnp.float32),
            jax.ShapeDtypeStruct((1, BLOCKS), jnp.int32),
            jax.ShapeDtypeStruct((1, 1), jnp.int32),
            jax.ShapeDtypeStruct((DEVICES, 1, DEVICES), jnp.float32),
        ),
        in_specs=[WHOLE, pl.BlockSpec(memory_space=pl.ANY)] + [WHOLE] * 5,
        out_specs=(WHOLE, WHOLE, SCALARS, WHOLE),
        scratch_shapes=[
            *[pltpu.VMEM((2 * BLOCKS * PIECE, LANES), jnp.float32)] * 3,
            *[pltpu.VMEM((4 * cap * PIECE, LANES), jnp.float32)] * 9,
            pltpu.VMEM((3, BLOCKS * PIECE, LANES), jnp.float32),
            pltpu.VMEM((3, 3, cap * PIECE, LANES), jnp.float32),
            pltpu.VMEM((ROWS, BLOCKS * LANES), jnp.float32),
            pltpu.VMEM((12, 4, 256), jnp.int32),
            *[pltpu.SMEM((4, 256), jnp.int32)] * 12,
            dma((CHUNKS,)), dma((12,)), dma((4, 3)), dma((4, 3)), dma((3, CHUNKS)), dma((3, CHUNKS)),
            dma((3, 3, 3)), dma((3, 3, 3)), dma((3,)), dma((3,)),
        ],
        compiler_params=pltpu.CompilerParams(collective_id=1, has_side_effects=True, vmem_limit_bytes=60 * 1024 * 1024),
    )(block_part.reshape(1, BLOCKS), states, *[v.reshape(1, ROWS - 1) for v in values])
    fits = longest[0, 0] <= cap
    return lax.cond(fits, settle, direct_route, parts, where.reshape(BLOCKS), counts, states, block_part, tile_perm, *values)


def solution(mesh):
    split = P(None, AXES)
    placed = (split, P(AXES), P(AXES, None), P(), P(), P(), P(), P())
    return jax.shard_map(on_device, mesh=mesh, in_specs=placed, out_specs=split, check_vma=False)
```

time: 210 us -> 135 us (0.64)
  blocking collectives: 34.8 us -> 0 us
  other arithmetic: 16.5 us -> 0 us
  local copies, waits for them, and re-layouts: 13.3 us -> 0.03 us
  matrix products: 8.93 us -> 0 us
  between operations: 6.01 us -> 0.73 us
  Pallas kernels: 127 us -> 132 us
    all_gather x2 -> x0, blocking collectives: 34.8 us -> none  [the longest x1 18.7 us: on_device(): counts = lax.all_gather(counts, 'group').reshape(DEVICES, DEVICES)]
    dot_general x33 -> x0, matrix products: 8.93 us -> none  [the longest x12 3.06 us: index_lists(): base = lax.dot(earlier.astype(jnp.float32), n).astype(jnp.int32)]
    reduce_sum x46 -> x0, other arithmetic: 7 us -> none  [the longest x38 4.22 us: index_lists(): out.append(j + jnp.sum(jnp.where(inside, shift, 0), axis=0, keepdims=True))]
    reduce_max x9 -> x0, other arithmetic: 5.65 us -> none  [longest_list(): longest.append(jnp.max(jnp.sum(grid, axis=axes)))]
    pallas_call x2, Pallas kernels: 127 us -> 132 us  [the longest x1 121 us: on_device(): pl.pallas_call(functools.partial(move_kernel, cap), out_shape=(jax.ShapeD...]
    concatenate x1 -> x0, local copies, waits for them, and re-layouts: 3.7 us -> none  [staged_route(): lists = jnp.concatenate(lists, axis=0)]
    another operation x1 -> x0, local copies, waits for them, and re-layouts: 2.71 us -> none  [longest_list(): grid = counts.reshape(SIZES + SIZES)]
    unnamed x6 -> x14, local copies, waits for them, and re-layouts: 2.71 us -> 0.03 us
where the time goes in v3:
time: 135 us; the launch traced here: 132 us
  Pallas kernels  132 us (98%)
    pallas_call x1, Pallas kernels, on_device(): pl.pallas_call(functools.partial(move_kernel, cap), out_shape=(jax.ShapeD...  121 us
    pallas_call x1, Pallas kernels, settle(): pl.pallas_call(functools.partial(settle_kernel, per), grid=(BLOCKS // per...  10.6 us

profile of v3, /device:TPU:5, one launch (start us, length us, event | category | flops | bytes accessed | tf_op | source)
XLA Modules:
  0.0 132.4 jit_solution(14751914424423502047)
XLA Ops:
  0.0 0.0 copy-start.2
  0.0 0.0 copy-start.5
  0.0 0.0 copy-start.7
  0.0 0.0 copy-start.6
  0.0 0.0 copy-start.3
  0.0 0.0 copy-start.4
  0.0 0.0 copy-start.1
  0.0 121.0 %shard_map.84 = (f32[2,3,1792,128]{3,2,1,0:T(8,128)}, s32[1,256]{1,0:T(1,128)S(1)}, s32[1,1]{1,0:T(1,128)}, f32[128,1,128]{2,1,0:T(1,128)S(1)}) custom-call(s32[1,256]{1,0:T(1,128)} %bitcast.17, f32[41,32768]{1,0:T(8,128)} %states_ref.1, f32[1,40]{1,0:T(1,128)} %bitcast.20, f32[1,40]{1,0:T(1,128)} %bitcast.23, f32[1,40]{1,0:T(1,128)} %bitcast.21, ...), custom_call_target="tpu_custom_call" | custom-call | tf_op jit(solution)/shard_map/pallas_call | solution.py:374
  121.7 0.0 copy-done.2
  121.7 0.0 copy-done.5
  121.7 0.0 copy-done.7
  121.7 0.0 copy-done.6
  121.7 0.0 copy-done.3
  121.7 0.0 copy-done.4
  121.7 0.0 copy-done.1
  121.7 10.6 %conditional.1 = (f32[41,32768]{1,0:T(8,128)}) conditional(s32[]{:T(128)} %bitcast.10, (s32[256]{0:T(256)S(1)}, f32[128,1,128]{2,1,0:T(1,128)S(1)}, f32[40]{0:T(128)S(1)}, f32[40]{0:T(128)S(1)}, f32[40]{0:T(128)S(1)}, /*index=5*/f32[40]{0:T(128)S(1)}, f32[40]{0:T(128)S(1)}, f32[41,32768]{1,0:T(8,128)}, s32[256,128]{1,0:T(8,128)S(1)}) %tuple.26, ...), branch_computations={%region_0.3_spmd, %region_3.4_spmd} | conditional | flops 17056590 | bytes 75939112 | solution.py:398
  121.8 10.6 %branch_1_fun.1 = f32[41,32768]{1,0:T(8,128)} custom-call(s32[256]{0:T(256)S(1)} %bitcast.22, f32[2,3,1792,128]{3,2,1,0:T(8,128)} %get-tuple-element.43.parts_ref, s32[256,128]{1,0:T(8,128)S(1)} %get-tuple-element.44.perm_ref), custom_call_target="tpu_custom_call" | custom-call | tf_op jit(solution)/shard_map/cond/branch_1_fun/pallas_call | solution.py:361
Async XLA Ops:
  0.0 121.7 %copy-start.2 = (s32[256]{0:T(256)S(1)}, s32[256]{0:T(256)}, u32[]{:S(2)}) copy-start(s32[256]{0:T(256)} %param.11) | copy-start | bytes 3076
  0.0 121.7 %copy-start.5 = (f32[40]{0:T(128)S(1)}, f32[40]{0:T(128)}, u32[]{:S(2)}) copy-start(f32[40]{0:T(128)} %param.13) | copy-start | bytes 484
  0.0 121.7 %copy-start.7 = (f32[40]{0:T(128)S(1)}, f32[40]{0:T(128)}, u32[]{:S(2)}) copy-start(f32[40]{0:T(128)} %param.14) | copy-start | bytes 484
  0.0 121.7 %copy-start.6 = (f32[40]{0:T(128)S(1)}, f32[40]{0:T(128)}, u32[]{:S(2)}) copy-start(f32[40]{0:T(128)} %param.15) | copy-start | bytes 484
  0.0 121.7 %copy-start.3 = (f32[40]{0:T(128)S(1)}, f32[40]{0:T(128)}, u32[]{:S(2)}) copy-start(f32[40]{0:T(128)} %param.16) | copy-start | bytes 484
  0.0 121.7 %copy-start.4 = (f32[40]{0:T(128)S(1)}, f32[40]{0:T(128)}, u32[]{:S(2)}) copy-start(f32[40]{0:T(128)} %param.17) | copy-start | bytes 484
  0.0 121.7 %copy-start.1 = (s32[256,128]{1,0:T(8,128)S(1)}, s32[256,128]{1,0:T(8,128)}, u32[]{:S(2)}) copy-start(s32[256,128]{1,0:T(8,128)} %param.12) | copy-start | bytes 393220

commit v4 on v3

--- a/solution.py
+++ b/solution.py
@@ -14,8 +14,10 @@
 ROWS = 41
 SLOTS = 4
 TIME_STEP = 0.25
-PIECE = 7
-LIMIT = 176
+PIECES = (4, 3)
+HALF = 21
+SETTLED = 24
+LIMITS = (176, 184, 176)
 SIZES = (4, 2, 4, 4)
 STRIDES = (32, 16, 4, 1)
 CORE = 1
@@ -52,9 +54,7 @@
     return slab, part, p[held_by]
 
 
-def index_lists(stage, order, own, counts, cap):
-    lists = 2 if stage == 3 else 4
-    size = 256 // lists
+def find_bases(stage, order, own, counts):
     col = lax.broadcasted_iota(jnp.int32, (256, 1), 0)
     row = lax.broadcasted_iota(jnp.int32, (1, 256), 1)
     slab, part, held = cells(stage, order, own, col)
@@ -66,15 +66,21 @@
     wide = jnp.broadcast_to(n, (256, LANES))
     earlier = (held_r == held) & (part_r * DEVICES + slab_r < part * DEVICES + slab)
     base = jnp.dot(earlier.astype(jnp.float32), wide, preferred_element_type=jnp.float32)[:, 0:1].astype(jnp.int32)
-    base = base + held * (BLOCKS if stage == 0 else cap)
-    shift = size.bit_length() - 1
-    ahead = ((row >> shift) == (col >> shift)) & (row < col)
+    return n, wide, base + held * (BLOCKS if stage == 0 else LIMITS[stage - 1])
+
+
+def index_lists(stage, order, own, counts):
+    size = 64
+    n, wide, base = find_bases(stage, order, own, counts)
+    col = lax.broadcasted_iota(jnp.int32, (256, 1), 0)
+    row = lax.broadcasted_iota(jnp.int32, (1, 256), 1)
+    ahead = ((row >> 6) == (col >> 6)) & (row < col)
     place = jnp.dot(ahead.astype(jnp.float32), wide, preferred_element_type=jnp.float32)[:, 0:1].astype(jnp.int32)
     end = place + n.astype(jnp.int32)
     gap = base - place
-    limit = 2 * BLOCKS - 1 if stage == 0 else 4 * cap - 1
+    limit = 2 * BLOCKS - 1 if stage == 0 else 4 * LIMITS[stage - 1] - 1
     out = []
-    for k in range(lists):
+    for k in range(4):
         one = slice(k * size, (k + 1) * size)
         inside = (row >= place[one]) & (row < end[one])
         found = row + jnp.sum(jnp.where(inside, gap[one], 0), axis=0, keepdims=True)
@@ -82,6 +88,11 @@
     return out
 
 
+def final_list(base, onehot, before):
+    found = jnp.sum(onehot * (before + base.astype(jnp.float32)), axis=0, keepdims=True).astype(jnp.int32)
+    return jnp.clip(found, 0, 4 * LIMITS[2] - 1)
+
+
 def same_key(dims):
     i = lax.broadcasted_iota(jnp.int32, (DEVICES, DEVICES), 0)
     j = lax.broadcasted_iota(jnp.int32, (DEVICES, DEVICES), 1)
@@ -89,13 +100,14 @@
     return ((i & mask) == (j & mask)).astype(jnp.float32)
 
 
-def longest_list(counts):
+def excess_of_longest(counts):
     longest = None
     for order in ORDERS:
         for stage in range(3):
             to, left = order[:stage + 1], order[stage:]
             sums = jnp.dot(same_key(to), counts, preferred_element_type=jnp.float32)
             sums = jnp.dot(sums, same_key(left), preferred_element_type=jnp.float32)
+            sums = sums - LIMITS[stage]
             longest = sums if longest is None else jnp.maximum(longest, sums)
     return jnp.max(longest, axis=0, keepdims=True)
 
@@ -121,11 +133,26 @@
 CHUNK = BLOCKS // CHUNKS
 
 
-def move_kernel(cap, part_ref, states_ref, hv, st, gr, co, re, out_ref, where_ref, longest_ref, counts_ref, *scratch):
-    adv, recv, stage, send = scratch[:3], (scratch[3:6], scratch[6:9], scratch[9:12]), scratch[12], scratch[13]
-    states, tables, lists = scratch[14], scratch[15], scratch[16:28]
+def first_row(w, t):
+    return t * PIECES[0] if w == 0 else 3 * PIECES[0] + t * PIECES[1]
+
+
+def move_kernel(part_ref, states_ref, hv, st, gr, co, re, out_ref, longest_ref, counts_ref, *scratch):
+    scratch = list(scratch)
+
+    def take(count):
+        taken = scratch[:count]
+        del scratch[:count]
+        return taken
+
+    adv = [take(3) for w in range(2)]
+    recv = [[take(3) for w in range(2)] for ph in range(3)]
+    stage, send = take(2), take(2)
+    states, tables = take(2)
+    lists = take(12)
+    settled, given, other_part = take(3)
     (load_sem, table_sem, count_send, count_recv, swap_send, swap_recv, send_sem, recv_sem,
-     last_send, last_recv) = scratch[28:]
+     last_send, last_recv, part_send, part_recv, store_sem) = scratch
     me = lax.axis_index("group") * 16 + lax.axis_index("peer")
     own = digits_of(me)
     core = own[CORE]
@@ -149,13 +176,19 @@
         pl.semaphore_signal(barrier, inc=1, device_id=along(d, delta), device_id_type=MESH)
 
     parts = part_ref[...]
-    onehot = (lax.broadcasted_iota(jnp.int32, (DEVICES, BLOCKS), 0) == parts).astype(jnp.float32)
+    number = lax.broadcasted_iota(jnp.int32, (DEVICES, BLOCKS), 0)
+    onehot = (number == parts).astype(jnp.float32)
     ones = jnp.ones((8, BLOCKS), jnp.float32)
     mine = lax.dot_general(ones, onehot, (((1,), (1,)), ((), ())), preferred_element_type=jnp.float32)[0:1]
     counts_ref[me] = mine
     params = [column(r[...]) for r in (hv, st, gr, co, re)]
 
     pl.semaphore_wait(barrier, len(neighbours))
+
+    part_swap = pltpu.make_async_remote_copy(
+        src_ref=part_ref, dst_ref=other_part, send_sem=part_send, recv_sem=part_recv,
+        device_id=along(CORE, 1), device_id_type=MESH)
+    part_swap.start()
 
     spread = (3, 2, 1, 0)
 
@@ -167,28 +200,29 @@
             send_sem=count_send.at[k, delta - 1], recv_sem=count_recv.at[k, delta - 1],
             device_id=along(spread[k], delta), device_id_type=MESH)
 
-    half = 3 * PIECE
-    mine_at = core * (BLOCKS * PIECE)
 
     def update(i, carry):
         for u in range(8):
             b = i * 8 + u
             new = advance(states[:, pl.ds(pl.multiple_of(b * LANES, LANES), LANES)], *params)
-            low = new[0:half]
-            high = jnp.concatenate([new[half:ROWS], new[ROWS - 1:ROWS]], axis=0)
+            low = jnp.concatenate([new[0:16], new[32:37]], axis=0)
+            high = jnp.concatenate([new[16:32], new[40:41], new[40:41], new[37:40]], axis=0)
             keep = jnp.where(core == 0, low, high)
             give = jnp.where(core == 0, high, low)
-            for t in range(3):
-                adv[t][pl.ds(mine_at + b * PIECE, PIECE), :] = keep[t * PIECE:(t + 1) * PIECE]
-                stage[t, pl.ds(b * PIECE, PIECE), :] = give[t * PIECE:(t + 1) * PIECE]
+            for w, size in enumerate(PIECES):
+                for t in range(3):
+                    first = first_row(w, t)
+                    adv[w][t][pl.ds((core * BLOCKS + b) * size, size), :] = keep[first:first + size]
+                    stage[w][t, pl.ds(b * size, size), :] = give[first:first + size]
         return carry
 
-    def swap(t, k):
-        rows = CHUNK * PIECE
+    def swap(w, t, k):
+        rows = CHUNK * PIECES[w]
+        mine_at = core * (BLOCKS * PIECES[w])
         return pltpu.make_async_remote_copy(
-            src_ref=stage.at[t, pl.ds(k * rows, rows)],
-            dst_ref=adv[t].at[pl.ds(pl.multiple_of(mine_at + k * rows, 8), rows)],
-            send_sem=swap_send.at[t, k], recv_sem=swap_recv.at[t, k],
+            src_ref=stage[w].at[t, pl.ds(k * rows, rows)],
+            dst_ref=adv[w][t].at[pl.ds(pl.multiple_of(mine_at + k * rows, 8), rows)],
+            send_sem=swap_send.at[w, t, k], recv_sem=swap_recv.at[w, t, k],
             device_id=along(CORE, 1), device_id_type=MESH)
 
     for k in range(CHUNKS):
@@ -196,8 +230,9 @@
             tell(k, delta).start()
         load(k).wait()
         lax.fori_loop(k * CHUNK // 8, (k + 1) * CHUNK // 8, update, 0)
-        for t in range(3):
-            swap(t, k).start()
+        for w in range(2):
+            for t in range(3):
+                swap(w, t, k).start()
         for delta in range(1, SIZES[spread[k]]):
             tell(k, delta).wait()
 
@@ -207,8 +242,7 @@
         return pltpu.make_async_copy(tables.at[ph * 3 + t], lists[ph * 3 + t], table_sem.at[ph * 3 + t])
 
     def make_table(ph, t):
-        found = index_lists(ph, ORDERS[t], own, counts, cap)
-        for k, one in enumerate(found):
+        for k, one in enumerate(index_lists(ph, ORDERS[t], own, counts)):
             tables[ph * 3 + t, k:k + 1, :] = one
 
     for t in range(3):
@@ -216,80 +250,126 @@
     for t in range(3):
         table(0, t).start()
 
-    def hop(t, ph, delta):
+    def hop(w, t, ph, delta):
         dim = ORDERS[t][ph]
+        rows = LIMITS[ph] * PIECES[w]
         return pltpu.make_async_remote_copy(
-            src_ref=send.at[t, delta - 1],
-            dst_ref=recv[ph][t].at[pl.ds(pl.multiple_of(own[dim] * (cap * PIECE), 8), cap * PIECE)],
-            send_sem=send_sem.at[ph, t, delta - 1], recv_sem=recv_sem.at[ph, t, delta - 1],
+            src_ref=send[w].at[t, delta - 1, pl.ds(0, rows)],
+            dst_ref=recv[ph][w][t].at[pl.ds(pl.multiple_of(own[dim] * rows, 8), rows)],
+            send_sem=send_sem.at[ph, w, t, delta - 1], recv_sem=recv_sem.at[ph, w, t, delta - 1],
             device_id=along(dim, delta), device_id_type=MESH)
 
-    def gather(source, target, start, which, row, count):
+    def gather(w, source, target, start, which, row, count):
+        size = PIECES[w]
+
         def body(i, carry):
             for u in range(8):
                 j = i * 8 + u
-                target[pl.ds(start + j * PIECE, PIECE), :] = source[pl.ds(which[row, j] * PIECE, PIECE), :]
+                target[pl.ds(start + j * size, size), :] = source[pl.ds(which[row, j] * size, size), :]
             return carry
 
         lax.fori_loop(0, count // 8, body, 0)
+
+    def settle_piece(w, t, target, row, begin, end):
+        size = PIECES[w]
+        first = first_row(w, t)
+        if first == HALF - size:
+            first = first + size * core
+        source, which = recv[2][w][t], lists[9 + t]
+
+        def body(i, carry):
+            for u in range(8):
+                j = i * 8 + u
+                target[j, pl.ds(first, size), :] = source[pl.ds(which[row, j] * size, size), :]
+            return carry
+
+        lax.fori_loop(begin // 8, end // 8, body, 0)
+
+    def send_off(w, ph):
+        sources = []
+        for t in range(3):
+            if ph == 0:
+                for k in range(CHUNKS):
+                    swap(w, t, k).wait()
+                sources.append(adv[w][t])
+            else:
+                for delta in (2, 1, 3):
+                    hop(w, t, ph - 1, delta).wait()
+                sources.append(recv[ph - 1][w][t])
+        for delta in (2, 1, 3, 0):
+            for t in range(3):
+                dim = ORDERS[t][ph]
+                to = lax.rem(own[dim] + delta, 4)
+                if delta:
+                    gather(w, sources[t], send[w].at[t, delta - 1], 0, lists[ph * 3 + t], to, LIMITS[ph])
+                    hop(w, t, ph, delta).start()
+                else:
+                    start = own[dim] * (LIMITS[ph] * PIECES[w])
+                    gather(w, sources[t], recv[ph][w][t], start, lists[ph * 3 + t], to, LIMITS[ph])
 
     for ph in range(3):
         for t in range(3):
-            dim = ORDERS[t][ph]
             table(ph, t).wait()
-            if ph == 0:
-                for k in range(CHUNKS):
-                    swap(t, k).wait()
-                source = adv[t]
-            else:
-                for delta in (2, 1, 3):
-                    hop(t, ph - 1, delta).wait()
-                source = recv[ph - 1][t]
-            for delta in (2, 1, 3, 0):
-                to = lax.rem(own[dim] + delta, 4)
-                if delta:
-                    gather(source, send.at[t, delta - 1], 0, lists[ph * 3 + t], to, cap)
-                    hop(t, ph, delta).start()
-                else:
-                    gather(source, recv[ph][t], own[dim] * (cap * PIECE), lists[ph * 3 + t], to, cap)
-        for t in range(3):
-            make_table(ph + 1, t)
+        for w in range(2):
+            send_off(w, ph)
+        if ph < 2:
+            for t in range(3):
+                make_table(ph + 1, t)
+        else:
+            part_swap.wait()
+            theirs = (number == other_part[...]).astype(jnp.float32)
+            r = lax.broadcasted_iota(jnp.int32, (BLOCKS, BLOCKS), 0)
+            c = lax.broadcasted_iota(jnp.int32, (BLOCKS, BLOCKS), 1)
+            earlier = (r < c).astype(jnp.float32)
+            before = jnp.dot(onehot, earlier, preferred_element_type=jnp.float32)
+            before_theirs = jnp.dot(theirs, earlier, preferred_element_type=jnp.float32)
+            for t in range(3):
+                base = find_bases(3, ORDERS[t], own, counts)[2]
+                low, high = base[0:DEVICES], base[DEVICES:2 * DEVICES]
+                tables[9 + t, 0:1, :] = final_list(jnp.where(core == 0, low, high), onehot, before)
+                tables[9 + t, 1:2, :] = final_list(jnp.where(core == 0, high, low), theirs, before_theirs)
         for t in range(3):
             table(ph + 1, t).start()
         if ph == 0:
-            longest_ref[0, 0] = jnp.max(longest_list(counts)).astype(jnp.int32)
-            r = lax.broadcasted_iota(jnp.int32, (BLOCKS, BLOCKS), 0)
-            c = lax.broadcasted_iota(jnp.int32, (BLOCKS, BLOCKS), 1)
-            before = jnp.dot(onehot, (r < c).astype(jnp.float32), preferred_element_type=jnp.float32)
-            d = lax.broadcasted_iota(jnp.int32, (DEVICES, DEVICES), 0)
-            e = lax.broadcasted_iota(jnp.int32, (DEVICES, DEVICES), 1)
-            ahead = jnp.sum(jnp.where(e < d, mine, 0.0), axis=1, keepdims=True)
-            where_ref[...] = jnp.sum(onehot * (before + ahead), axis=0, keepdims=True).astype(jnp.int32)
-
-    def last(t):
+            longest_ref[0, 0] = jnp.max(excess_of_longest(counts)).astype(jnp.int32)
+
+    pieces = ((0, BLOCKS, 0, 8), (0, BLOCKS // 2, 8, 16), (BLOCKS // 2, BLOCKS // 2, 8, 16))
+
+    def last(k):
+        b, n, r, m = pieces[k]
         return pltpu.make_async_remote_copy(
-            src_ref=stage.at[t], dst_ref=out_ref.at[core, t],
-            send_sem=last_send.at[t], recv_sem=last_recv.at[t],
+            src_ref=given.at[pl.ds(b, n), pl.ds(r, m)], dst_ref=out_ref.at[core, pl.ds(b, n), pl.ds(r, m)],
+            send_sem=last_send.at[k], recv_sem=last_recv.at[k],
             device_id=along(CORE, 1), device_id_type=MESH)
+
+    def store(k):
+        b, n, r, m = pieces[k]
+        return pltpu.make_async_copy(
+            settled.at[pl.ds(b, n), pl.ds(r, m)], out_ref.at[core, pl.ds(b, n), pl.ds(r, m)], store_sem.at[k])
 
     for t in range(3):
         table(3, t).wait()
-        for delta in (2, 1, 3):
-            hop(t, 2, delta).wait()
-        gather(recv[2][t], stage.at[t], 0, lists[9 + t], 1 - core, BLOCKS)
-        last(t).start()
-    for t in range(3):
-        gather(recv[2][t], out_ref.at[core, t], 0, lists[9 + t], core, BLOCKS)
-    for t in range(3):
-        last(t).wait()
-
-
-def settle_kernel(per_step, where_ref, parts_ref, perm_ref, out_ref):
-    step = pl.program_id(0)
+    for w in range(2):
+        for t in range(3):
+            for delta in (2, 1, 3):
+                hop(w, t, 2, delta).wait()
+        runs = ((0, 0, BLOCKS),) if w == 0 else ((1, 0, BLOCKS // 2), (2, BLOCKS // 2, BLOCKS))
+        for target, row, copy in ((given, 1, last), (settled, 0, store)):
+            for k, begin, end in runs:
+                for t in range(3):
+                    settle_piece(w, t, target, row, begin, end)
+                copy(k).start()
+    for k in range(3):
+        last(k).wait()
+        store(k).wait()
+
+
+def settle_kernel(per_step, parts_ref, perm_ref, out_ref):
+    early = lax.broadcasted_iota(jnp.int32, (8, LANES), 0) < 5
     for j in range(per_step):
-        at = where_ref[step * per_step + j] * PIECE
-        rows = [parts_ref[h, t, pl.ds(at, PIECE), :] for h in range(2) for t in range(3)]
-        block = jnp.concatenate(rows, axis=0)[0:ROWS]
+        low, high = parts_ref[0, j], parts_ref[1, j]
+        mixed = jnp.where(early, low[16:24], high[16:24])
+        block = jnp.concatenate([low[0:16], high[0:16], mixed, high[16:17]], axis=0)
         index = jnp.broadcast_to(perm_ref[j:j + 1, :], (ROWS, LANES))
         out_ref[:, j * LANES:(j + 1) * LANES] = jnp.take_along_axis(block, index, axis=1)
 
@@ -324,7 +404,7 @@
 SCALARS = pl.BlockSpec(memory_space=pltpu.SMEM)
 
 
-def direct_route(parts, where, counts, states, block_part, tile_perm, *values):
+def direct_route(parts, counts, states, block_part, tile_perm, *values):
     me = lax.axis_index(AXES)
     number = jnp.arange(DEVICES, dtype=jnp.int32)
     onehot = (block_part[:, None] == number[None, :]).astype(jnp.float32)
@@ -356,46 +436,50 @@
     )(block_part * SLOTS + rank, arrived, tile_perm)
 
 
-def settle(parts, where, counts, states, block_part, tile_perm, *values):
-    per = 16
+def settle(parts, counts, states, block_part, tile_perm, *values):
+    per = 32
     return pl.pallas_call(
         functools.partial(settle_kernel, per),
         grid=(BLOCKS // per,),
         out_shape=jax.ShapeDtypeStruct((ROWS, BLOCKS * LANES), jnp.float32),
-        in_specs=[SCALARS, WHOLE, pl.BlockSpec((per, LANES), lambda i: (i, 0))],
+        in_specs=[
+            pl.BlockSpec((2, per, SETTLED, LANES), lambda i: (0, i, 0, 0)),
+            pl.BlockSpec((per, LANES), lambda i: (i, 0)),
+        ],
         out_specs=pl.BlockSpec((ROWS, per * LANES), lambda i: (0, i)),
         compiler_params=pltpu.CompilerParams(vmem_limit_bytes=60 * 1024 * 1024),
-    )(where, parts, tile_perm)
+    )(parts, tile_perm)
 
 
 def on_device(states, block_part, tile_perm, *values):
-    cap = LIMIT
     dma = pltpu.SemaphoreType.DMA
-    parts, where, longest, counts = pl.pallas_call(
-        functools.partial(move_kernel, cap),
+    parts, longest, counts = pl.pallas_call(
+        move_kernel,
         out_shape=(
-            jax.ShapeDtypeStruct((2, 3, BLOCKS * PIECE, LANES), jnp.float32),
-            jax.ShapeDtypeStruct((1, BLOCKS), jnp.int32),
+            jax.ShapeDtypeStruct((2, BLOCKS, SETTLED, LANES), jnp.float32),
             jax.ShapeDtypeStruct((1, 1), jnp.int32),
             jax.ShapeDtypeStruct((DEVICES, 1, DEVICES), jnp.float32),
         ),
         in_specs=[WHOLE, pl.BlockSpec(memory_space=pl.ANY)] + [WHOLE] * 5,
-        out_specs=(WHOLE, WHOLE, SCALARS, WHOLE),
+        out_specs=(pl.BlockSpec(memory_space=pl.ANY), SCALARS, WHOLE),
         scratch_shapes=[
-            *[pltpu.VMEM((2 * BLOCKS * PIECE, LANES), jnp.float32)] * 3,
-            *[pltpu.VMEM((4 * cap * PIECE, LANES), jnp.float32)] * 9,
-            pltpu.VMEM((3, BLOCKS * PIECE, LANES), jnp.float32),
-            pltpu.VMEM((3, 3, cap * PIECE, LANES), jnp.float32),
+            *[pltpu.VMEM((2 * BLOCKS * n, LANES), jnp.float32) for n in PIECES for t in range(3)],
+            *[pltpu.VMEM((4 * limit * n, LANES), jnp.float32) for limit in LIMITS for n in PIECES for t in range(3)],
+            *[pltpu.VMEM((3, BLOCKS * n, LANES), jnp.float32) for n in PIECES],
+            *[pltpu.VMEM((3, 3, max(LIMITS) * n, LANES), jnp.float32) for n in PIECES],
             pltpu.VMEM((ROWS, BLOCKS * LANES), jnp.float32),
             pltpu.VMEM((12, 4, 256), jnp.int32),
             *[pltpu.SMEM((4, 256), jnp.int32)] * 12,
-            dma((CHUNKS,)), dma((12,)), dma((4, 3)), dma((4, 3)), dma((3, CHUNKS)), dma((3, CHUNKS)),
-            dma((3, 3, 3)), dma((3, 3, 3)), dma((3,)), dma((3,)),
+            pltpu.VMEM((BLOCKS, SETTLED, LANES), jnp.float32),
+            pltpu.VMEM((BLOCKS, SETTLED, LANES), jnp.float32),
+            pltpu.VMEM((1, BLOCKS), jnp.int32),
+            dma((CHUNKS,)), dma((12,)), dma((4, 3)), dma((4, 3)), dma((2, 3, CHUNKS)), dma((2, 3, CHUNKS)),
+            dma((3, 2, 3, 3)), dma((3, 2, 3, 3)), dma((3,)), dma((3,)), dma, dma, dma((3,)),
         ],
         compiler_params=pltpu.CompilerParams(collective_id=1, has_side_effects=True, vmem_limit_bytes=60 * 1024 * 1024),
     )(block_part.reshape(1, BLOCKS), states, *[v.reshape(1, ROWS - 1) for v in values])
-    fits = longest[0, 0] <= cap
-    return lax.cond(fits, settle, direct_route, parts, where.reshape(BLOCKS), counts, states, block_part, tile_perm, *values)
+    fits = longest[0, 0] <= 0
+    return lax.cond(fits, settle, direct_route, parts, counts, states, block_part, tile_perm, *values)
 
 
 def solution(mesh):

time: 135 us -> 126 us (0.933)
  the two profiles are of different devices: /device:TPU:5 before, /device:TPU:1 now
where the time goes in v4:
time: 126 us
  Pallas kernels  125 us (99%)
    pallas_call x1, Pallas kernels, on_device(): pl.pallas_call(move_kernel, out_shape=(jax.ShapeDtypeStruct((2, BLOCKS, S...  116 us
    pallas_call x1, Pallas kernels, settle(): pl.pallas_call(functools.partial(settle_kernel, per), grid=(BLOCKS // per...  9.01 us

profile of v4, /device:TPU:1, one launch (start us, length us, event | category | flops | bytes accessed | tf_op | source)
XLA Modules:
  0.0 125.6 jit_solution(7472106188999482225)
XLA Ops:
  0.0 0.0 copy-start.2
  0.0 0.0 copy-start.5
  0.0 0.0 copy-start.7
  0.0 0.0 copy-start.6
  0.0 0.0 copy-start.3
  0.0 0.0 copy-start.4
  0.0 0.0 copy-start.1
  0.0 115.8 %shard_map.84 = (f32[2,256,24,128]{3,2,1,0:T(8,128)}, s32[1,1]{1,0:T(1,128)}, f32[128,1,128]{2,1,0:T(1,128)S(1)}) custom-call(s32[1,256]{1,0:T(1,128)} %bitcast.16, f32[41,32768]{1,0:T(8,128)} %states_ref.1, f32[1,40]{1,0:T(1,128)} %bitcast.19, f32[1,40]{1,0:T(1,128)} %bitcast.21, f32[1,40]{1,0:T(1,128)} %bitcast.20, f32[1,40]{1,0:T(1,128)} %bitcast.17, ...), custom_call_target="tpu_custom_call" | custom-call | tf_op jit(solution)/shard_map/pallas_call | solution.py:456
  116.5 0.0 copy-done.2
  116.5 0.0 copy-done.5
  116.5 0.0 copy-done.7
  116.5 0.0 copy-done.6
  116.5 0.0 copy-done.3
  116.5 0.0 copy-done.4
  116.5 0.0 copy-done.1
  116.5 9.0 %conditional.1 = (f32[41,32768]{1,0:T(8,128)}) conditional(s32[]{:T(128)} %bitcast.9, (s32[256]{0:T(256)S(1)}, f32[128,1,128]{2,1,0:T(1,128)S(1)}, f32[40]{0:T(128)S(1)}, f32[40]{0:T(128)S(1)}, f32[40]{0:T(128)S(1)}, /*index=5*/f32[40]{0:T(128)S(1)}, f32[40]{0:T(128)S(1)}, f32[41,32768]{1,0:T(8,128)}, s32[256,128]{1,0:T(8,128)S(1)}) %tuple.26, ...), branch_computations={%region_0.3_spmd, %region_3.4_spmd} | conditional | flops 17056590 | bytes 75939112 | solution.py:482
  116.5 9.0 %branch_1_fun.1 = f32[41,32768]{1,0:T(8,128)} custom-call(f32[2,256,24,128]{3,2,1,0:T(8,128)} %get-tuple-element.39.parts_ref, s32[256,128]{1,0:T(8,128)S(1)} %get-tuple-element.40.perm_ref), custom_call_target="tpu_custom_call" | custom-call | tf_op jit(solution)/shard_map/cond/branch_1_fun/pallas_call | solution.py:441
Async XLA Ops:
  0.0 116.5 %copy-start.2 = (s32[256]{0:T(256)S(1)}, s32[256]{0:T(256)}, u32[]{:S(2)}) copy-start(s32[256]{0:T(256)} %param.11) | copy-start | bytes 3076
  0.0 116.5 %copy-start.5 = (f32[40]{0:T(128)S(1)}, f32[40]{0:T(128)}, u32[]{:S(2)}) copy-start(f32[40]{0:T(128)} %param.13) | copy-start | bytes 484
  0.0 116.5 %copy-start.7 = (f32[40]{0:T(128)S(1)}, f32[40]{0:T(128)}, u32[]{:S(2)}) copy-start(f32[40]{0:T(128)} %param.14) | copy-start | bytes 484
  0.0 116.5 %copy-start.6 = (f32[40]{0:T(128)S(1)}, f32[40]{0:T(128)}, u32[]{:S(2)}) copy-start(f32[40]{0:T(128)} %param.15) | copy-start | bytes 484
  0.0 116.5 %copy-start.3 = (f32[40]{0:T(128)S(1)}, f32[40]{0:T(128)}, u32[]{:S(2)}) copy-start(f32[40]{0:T(128)} %param.16) | copy-start | bytes 484
  0.0 116.5 %copy-start.4 = (f32[40]{0:T(128)S(1)}, f32[40]{0:T(128)}, u32[]{:S(2)}) copy-start(f32[40]{0:T(128)} %param.17) | copy-start | bytes 484
  0.0 116.5 %copy-start.1 = (s32[256,128]{1,0:T(8,128)S(1)}, s32[256,128]{1,0:T(8,128)}, u32[]{:S(2)}) copy-start(s32[256,128]{1,0:T(8,128)} %param.12) | copy-start | bytes 393220

commit v5 on v4

--- a/solution.py
+++ b/solution.py
@@ -129,6 +129,8 @@
     return jnp.broadcast_to(picked, (ROWS, LANES))
 
 
+PLANE = [(0, 0, z, x) for z in range(4) for x in range(4) if z or x]
+COLUMN = [(y, c, 0, 0) for y in range(4) for c in range(2) if y or c]
 CHUNKS = 4
 CHUNK = BLOCKS // CHUNKS
 
@@ -160,9 +162,11 @@
     def at(coords):
         return (coords[0] * 2 + coords[CORE], coords[2] * 4 + coords[3])
 
+    def shifted(shift):
+        return at(tuple(lax.rem(own[d] + shift[d], SIZES[d]) if shift[d] else own[d] for d in range(4)))
+
     def along(dim, delta):
-        to = lax.rem(own[dim] + delta, SIZES[dim])
-        return at(tuple(to if d == dim else own[d] for d in range(4)))
+        return shifted(tuple(delta if d == dim else 0 for d in range(4)))
 
     def load(k):
         columns = pl.ds(k * CHUNK * LANES, CHUNK * LANES)
@@ -171,9 +175,8 @@
     for k in range(CHUNKS):
         load(k).start()
     barrier = pltpu.get_barrier_semaphore()
-    neighbours = [(d, delta) for d in range(4) for delta in range(1, SIZES[d])]
-    for d, delta in neighbours:
-        pl.semaphore_signal(barrier, inc=1, device_id=along(d, delta), device_id_type=MESH)
+    for shift in PLANE + COLUMN:
+        pl.semaphore_signal(barrier, inc=1, device_id=shifted(shift), device_id_type=MESH)
 
     parts = part_ref[...]
     number = lax.broadcasted_iota(jnp.int32, (DEVICES, BLOCKS), 0)
@@ -183,23 +186,20 @@
     counts_ref[me] = mine
     params = [column(r[...]) for r in (hv, st, gr, co, re)]
 
-    pl.semaphore_wait(barrier, len(neighbours))
+    pl.semaphore_wait(barrier, len(PLANE) + len(COLUMN))
 
     part_swap = pltpu.make_async_remote_copy(
         src_ref=part_ref, dst_ref=other_part, send_sem=part_send, recv_sem=part_recv,
         device_id=along(CORE, 1), device_id_type=MESH)
     part_swap.start()
 
-    spread = (3, 2, 1, 0)
-
-    def tell(k, delta):
-        held = STRIDES[spread[k]]
+    def tell(k, i):
+        held = 16 if k else 1
         rows = pl.ds(lax.div(me, held) * held, held)
         return pltpu.make_async_remote_copy(
             src_ref=counts_ref.at[rows], dst_ref=counts_ref.at[rows],
-            send_sem=count_send.at[k, delta - 1], recv_sem=count_recv.at[k, delta - 1],
-            device_id=along(spread[k], delta), device_id_type=MESH)
-
+            send_sem=count_send.at[k, i], recv_sem=count_recv.at[k, i],
+            device_id=shifted((PLANE, COLUMN)[k][i]), device_id_type=MESH)
 
     def update(i, carry):
         for u in range(8):
@@ -226,15 +226,21 @@
             device_id=along(CORE, 1), device_id_type=MESH)
 
     for k in range(CHUNKS):
-        for delta in range(1, SIZES[spread[k]]):
-            tell(k, delta).start()
+        if k == 0:
+            for i in range(len(PLANE)):
+                tell(0, i).start()
+        if k == CHUNKS - 1:
+            for i in range(len(PLANE)):
+                tell(0, i).wait()
+            for i in range(len(COLUMN)):
+                tell(1, i).start()
         load(k).wait()
         lax.fori_loop(k * CHUNK // 8, (k + 1) * CHUNK // 8, update, 0)
         for w in range(2):
             for t in range(3):
                 swap(w, t, k).start()
-        for delta in range(1, SIZES[spread[k]]):
-            tell(k, delta).wait()
+    for i in range(len(COLUMN)):
+        tell(1, i).wait()
 
     counts = counts_ref[...].reshape(DEVICES, DEVICES)
 
@@ -247,7 +253,6 @@
 
     for t in range(3):
         make_table(0, t)
-    for t in range(3):
         table(0, t).start()
 
     def hop(w, t, ph, delta):
@@ -437,7 +442,7 @@
 
 
 def settle(parts, counts, states, block_part, tile_perm, *values):
-    per = 32
+    per = 128
     return pl.pallas_call(
         functools.partial(settle_kernel, per),
         grid=(BLOCKS // per,),
@@ -473,7 +478,7 @@
             pltpu.VMEM((BLOCKS, SETTLED, LANES), jnp.float32),
             pltpu.VMEM((BLOCKS, SETTLED, LANES), jnp.float32),
             pltpu.VMEM((1, BLOCKS), jnp.int32),
-            dma((CHUNKS,)), dma((12,)), dma((4, 3)), dma((4, 3)), dma((2, 3, CHUNKS)), dma((2, 3, CHUNKS)),
+            dma((CHUNKS,)), dma((12,)), dma((2, 15)), dma((2, 15)), dma((2, 3, CHUNKS)), dma((2, 3, CHUNKS)),
             dma((3, 2, 3, 3)), dma((3, 2, 3, 3)), dma((3,)), dma((3,)), dma, dma, dma((3,)),
         ],
         compiler_params=pltpu.CompilerParams(collective_id=1, has_side_effects=True, vmem_limit_bytes=60 * 1024 * 1024),

time: 126 us -> 121 us (0.960)
  the two profiles are of different devices: /device:TPU:1 before, /device:TPU:5 now
where the time goes in v5:
time: 121 us; the launch traced here: 120 us
  Pallas kernels  119 us (98%)
    pallas_call x1, Pallas kernels, on_device(): pl.pallas_call(move_kernel, out_shape=(jax.ShapeDtypeStruct((2, BLOCKS, S...  113 us
    pallas_call x1, Pallas kernels, settle(): pl.pallas_call(functools.partial(settle_kernel, per), grid=(BLOCKS // per...  6.16 us

profile of v5, /device:TPU:5, one launch (start us, length us, event | category | flops | bytes accessed | tf_op | source)
XLA Modules:
  0.0 119.7 jit_solution(3593485884434991825)
XLA Ops:
  0.0 0.0 copy-start.2
  0.0 0.0 copy-start.5
  0.0 0.0 copy-start.7
  0.0 0.0 copy-start.6
  0.0 0.0 copy-start.3
  0.0 0.0 copy-start.4
  0.0 0.0 copy-start.1
  0.0 112.8 %shard_map.84 = (f32[2,256,24,128]{3,2,1,0:T(8,128)}, s32[1,1]{1,0:T(1,128)}, f32[128,1,128]{2,1,0:T(1,128)S(1)}) custom-call(s32[1,256]{1,0:T(1,128)} %bitcast.16, f32[41,32768]{1,0:T(8,128)} %states_ref.1, f32[1,40]{1,0:T(1,128)} %bitcast.19, f32[1,40]{1,0:T(1,128)} %bitcast.21, f32[1,40]{1,0:T(1,128)} %bitcast.20, f32[1,40]{1,0:T(1,128)} %bitcast.17, ...), custom_call_target="tpu_custom_call" | custom-call | tf_op jit(solution)/shard_map/pallas_call | solution.py:461
  113.5 0.0 copy-done.2
  113.5 0.0 copy-done.5
  113.5 0.0 copy-done.7
  113.5 0.0 copy-done.6
  113.5 0.0 copy-done.3
  113.5 0.0 copy-done.4
  113.5 0.0 copy-done.1
  113.5 6.2 %conditional.1 = (f32[41,32768]{1,0:T(8,128)}) conditional(s32[]{:T(128)} %bitcast.9, (s32[256]{0:T(256)S(1)}, f32[128,1,128]{2,1,0:T(1,128)S(1)}, f32[40]{0:T(128)S(1)}, f32[40]{0:T(128)S(1)}, f32[40]{0:T(128)S(1)}, /*index=5*/f32[40]{0:T(128)S(1)}, f32[40]{0:T(128)S(1)}, f32[41,32768]{1,0:T(8,128)}, s32[256,128]{1,0:T(8,128)S(1)}) %tuple.26, ...), branch_computations={%region_0.3_spmd, %region_3.4_spmd} | conditional | flops 17056590 | bytes 75939112 | solution.py:487
  113.5 6.2 %branch_1_fun.1 = f32[41,32768]{1,0:T(8,128)} custom-call(f32[2,256,24,128]{3,2,1,0:T(8,128)} %get-tuple-element.39.parts_ref, s32[256,128]{1,0:T(8,128)S(1)} %get-tuple-element.40.perm_ref), custom_call_target="tpu_custom_call" | custom-call | tf_op jit(solution)/shard_map/cond/branch_1_fun/pallas_call | solution.py:446
Async XLA Ops:
  0.0 113.5 %copy-start.2 = (s32[256]{0:T(256)S(1)}, s32[256]{0:T(256)}, u32[]{:S(2)}) copy-start(s32[256]{0:T(256)} %param.11) | copy-start | bytes 3076
  0.0 113.5 %copy-start.5 = (f32[40]{0:T(128)S(1)}, f32[40]{0:T(128)}, u32[]{:S(2)}) copy-start(f32[40]{0:T(128)} %param.13) | copy-start | bytes 484
  0.0 113.5 %copy-start.7 = (f32[40]{0:T(128)S(1)}, f32[40]{0:T(128)}, u32[]{:S(2)}) copy-start(f32[40]{0:T(128)} %param.14) | copy-start | bytes 484
  0.0 113.5 %copy-start.6 = (f32[40]{0:T(128)S(1)}, f32[40]{0:T(128)}, u32[]{:S(2)}) copy-start(f32[40]{0:T(128)} %param.15) | copy-start | bytes 484
  0.0 113.5 %copy-start.3 = (f32[40]{0:T(128)S(1)}, f32[40]{0:T(128)}, u32[]{:S(2)}) copy-start(f32[40]{0:T(128)} %param.16) | copy-start | bytes 484
  0.0 113.5 %copy-start.4 = (f32[40]{0:T(128)S(1)}, f32[40]{0:T(128)}, u32[]{:S(2)}) copy-start(f32[40]{0:T(128)} %param.17) | copy-start | bytes 484
  0.0 113.5 %copy-start.1 = (s32[256,128]{1,0:T(8,128)S(1)}, s32[256,128]{1,0:T(8,128)}, u32[]{:S(2)}) copy-start(s32[256,128]{1,0:T(8,128)} %param.12) | copy-start | bytes 393220

commit v6 on v5

--- a/solution.py
+++ b/solution.py
@@ -266,14 +266,15 @@
 
     def gather(w, source, target, start, which, row, count):
         size = PIECES[w]
+        step = 16 if count % 16 == 0 else 8
 
         def body(i, carry):
-            for u in range(8):
-                j = i * 8 + u
+            for u in range(step):
+                j = i * step + u
                 target[pl.ds(start + j * size, size), :] = source[pl.ds(which[row, j] * size, size), :]
             return carry
 
-        lax.fori_loop(0, count // 8, body, 0)
+        lax.fori_loop(0, count // step, body, 0)
 
     def settle_piece(w, t, target, row, begin, end):
         size = PIECES[w]
@@ -338,7 +339,7 @@
         if ph == 0:
             longest_ref[0, 0] = jnp.max(excess_of_longest(counts)).astype(jnp.int32)
 
-    pieces = ((0, BLOCKS, 0, 8), (0, BLOCKS // 2, 8, 16), (BLOCKS // 2, BLOCKS // 2, 8, 16))
+    pieces = ((0, BLOCKS, 0, 12), (0, BLOCKS // 2, 12, 12), (BLOCKS // 2, BLOCKS // 2, 12, 12))
 
     def last(k):
         b, n, r, m = pieces[k]

time: 121 us -> 121 us (level)
  no operation moved by 1% of the time
where the time goes in v6:
time: 121 us; the launch traced here: 119 us
  Pallas kernels  119 us (98%)
    pallas_call x1, Pallas kernels, on_device(): pl.pallas_call(move_kernel, out_shape=(jax.ShapeDtypeStruct((2, BLOCKS, S...  112 us
    pallas_call x1, Pallas kernels, settle(): pl.pallas_call(functools.partial(settle_kernel, per), grid=(BLOCKS // per...  6.16 us

profile of v6, /device:TPU:5, one launch (start us, length us, event | category | flops | bytes accessed | tf_op | source)
XLA Modules:
  0.0 119.3 jit_solution(17028818549745972409)
XLA Ops:
  0.0 0.0 copy-start.2
  0.0 0.0 copy-start.5
  0.0 0.0 copy-start.7
  0.0 0.0 copy-start.6
  0.0 0.0 copy-start.3
  0.0 0.0 copy-start.4
  0.0 0.0 copy-start.1
  0.0 112.4 %shard_map.84 = (f32[2,256,24,128]{3,2,1,0:T(8,128)}, s32[1,1]{1,0:T(1,128)}, f32[128,1,128]{2,1,0:T(1,128)S(1)}) custom-call(s32[1,256]{1,0:T(1,128)} %bitcast.16, f32[41,32768]{1,0:T(8,128)} %states_ref.1, f32[1,40]{1,0:T(1,128)} %bitcast.19, f32[1,40]{1,0:T(1,128)} %bitcast.21, f32[1,40]{1,0:T(1,128)} %bitcast.20, f32[1,40]{1,0:T(1,128)} %bitcast.17, ...), custom_call_target="tpu_custom_call" | custom-call | tf_op jit(solution)/shard_map/pallas_call | solution.py:462
  113.1 0.0 copy-done.2
  113.1 0.0 copy-done.5
  113.1 0.0 copy-done.7
  113.1 0.0 copy-done.6
  113.1 0.0 copy-done.3
  113.1 0.0 copy-done.4
  113.2 0.0 copy-done.1
  113.2 6.2 %conditional.1 = (f32[41,32768]{1,0:T(8,128)}) conditional(s32[]{:T(128)} %bitcast.9, (s32[256]{0:T(256)S(1)}, f32[128,1,128]{2,1,0:T(1,128)S(1)}, f32[40]{0:T(128)S(1)}, f32[40]{0:T(128)S(1)}, f32[40]{0:T(128)S(1)}, /*index=5*/f32[40]{0:T(128)S(1)}, f32[40]{0:T(128)S(1)}, f32[41,32768]{1,0:T(8,128)}, s32[256,128]{1,0:T(8,128)S(1)}) %tuple.26, ...), branch_computations={%region_0.3_spmd, %region_3.4_spmd} | conditional | flops 17056590 | bytes 75939112 | solution.py:488
  113.2 6.2 %branch_1_fun.1 = f32[41,32768]{1,0:T(8,128)} custom-call(f32[2,256,24,128]{3,2,1,0:T(8,128)} %get-tuple-element.39.parts_ref, s32[256,128]{1,0:T(8,128)S(1)} %get-tuple-element.40.perm_ref), custom_call_target="tpu_custom_call" | custom-call | tf_op jit(solution)/shard_map/cond/branch_1_fun/pallas_call | solution.py:447
Async XLA Ops:
  0.0 113.1 %copy-start.2 = (s32[256]{0:T(256)S(1)}, s32[256]{0:T(256)}, u32[]{:S(2)}) copy-start(s32[256]{0:T(256)} %param.11) | copy-start | bytes 3076
  0.0 113.1 %copy-start.5 = (f32[40]{0:T(128)S(1)}, f32[40]{0:T(128)}, u32[]{:S(2)}) copy-start(f32[40]{0:T(128)} %param.13) | copy-start | bytes 484
  0.0 113.1 %copy-start.7 = (f32[40]{0:T(128)S(1)}, f32[40]{0:T(128)}, u32[]{:S(2)}) copy-start(f32[40]{0:T(128)} %param.14) | copy-start | bytes 484
  0.0 113.1 %copy-start.6 = (f32[40]{0:T(128)S(1)}, f32[40]{0:T(128)}, u32[]{:S(2)}) copy-start(f32[40]{0:T(128)} %param.15) | copy-start | bytes 484
  0.0 113.1 %copy-start.3 = (f32[40]{0:T(128)S(1)}, f32[40]{0:T(128)}, u32[]{:S(2)}) copy-start(f32[40]{0:T(128)} %param.16) | copy-start | bytes 484
  0.0 113.1 %copy-start.4 = (f32[40]{0:T(128)S(1)}, f32[40]{0:T(128)}, u32[]{:S(2)}) copy-start(f32[40]{0:T(128)} %param.17) | copy-start | bytes 484
  0.0 113.1 %copy-start.1 = (s32[256,128]{1,0:T(8,128)S(1)}, s32[256,128]{1,0:T(8,128)}, u32[]{:S(2)}) copy-start(s32[256,128]{1,0:T(8,128)} %param.12) | copy-start | bytes 393220
